TPU v7x, 128 devices: a whole 4x4x4 slice. The times are simulated.
128 devices in a mesh: band: 32 (over y, x, core), sub: 4 (over z).
Axes of the slice: x: 4, y: 4, z: 4, core: 2. Of those that a mesh axis runs over, the one named last changes fastest.
Arguments:
- fields: bfloat16 [12, 4194304], P(None, ('band', 'sub')), may hold values from -1.5 to 6
- land_mask: int32 [4194304], P(('band', 'sub')), may hold values from 0 to 1
- intersection: bfloat16 [32768, 128, 128], P(('band', 'sub')), as said below
- send_slot: int32 [32768], P(('band', 'sub')), may hold values from 0 to 511, as said below
- target_block: int32 [32768], P(('band', 'sub')), may hold values from 0 to 15
- live_blocks: int32 [128], P(('band', 'sub')), may hold values from 192 to 256, as said below
Outputs:
- remapped: float32 [12, 262144], P(None, ('band', 'sub'))
Inputs may be any that keep to these rules, and one draw needn't show every extreme that they name: `send_slot`: within one device's 256 entries the values are distinct; value // 4 is the device that owns the block's target; in each device's entries some owner is named exactly 4 times and none more. `live_blocks`: some device has all 256 slots live in every draw. `intersection`: entries are positive.
All inputs are finite; a program needn't handle non-finite values.
Results may differ from a plain program's by a relative error of at most 0.0003.
Values may be sent and summed in bfloat16 or wider, within the bound.
A program may use at most 64 MiB of HBM per device.

v0:
```python
import functools

import jax
import jax.numpy as jnp
from jax import lax
from jax.sharding import Mesh
from jax.sharding import PartitionSpec as P

TB_DEV = 16
BAND_SUB = ("band_0", "band_1", "band_2", "sub")


def one_axis_at_a_time(array, axes):
    return functools.reduce(lax.psum, axes, array)


def body(fields, land_mask, intersection, send_slot, target_block, live_blocks):
    block_count = intersection.shape[0]
    block_cells = intersection.shape[1]
    field_count = fields.shape[0]
    devices = lax.axis_size(BAND_SUB)
    capacity = max(2, 2 * block_count // devices)
    positions = devices * capacity
    live_rows = (jnp.arange(block_count, dtype=jnp.int32) < live_blocks[0]).astype(jnp.int32)
    kept_mask = land_mask.reshape(block_count, block_cells) * live_rows[:, None]
    kept_half = kept_mask.astype(jnp.bfloat16)
    masked = fields.reshape(field_count, block_count, block_cells) * kept_half[None, :, :]
    totals = jnp.sum(masked.astype(jnp.float32), axis=(1, 2))
    land_count = jnp.sum(kept_mask.astype(jnp.float32))
    global_totals, global_count = (
        one_axis_at_a_time(totals, BAND_SUB),
        one_axis_at_a_time(land_count, BAND_SUB),
    )
    land_mean = global_totals / jnp.maximum(global_count, 1.0)
    stacked_fields = jnp.concatenate([masked.transpose(1, 0, 2), kept_half[:, None, :]], axis=1)
    target_buffer = jnp.zeros((positions,), jnp.int32).at[send_slot].set(target_block)
    contribution_partial = jnp.einsum(
        "myr,mrw->myw", stacked_fields, intersection, preferred_element_type=jnp.float32
    )
    partial_buffer = (
        jnp.zeros((positions, field_count + 1, block_cells), jnp.float32)
        .at[send_slot]
        .set(contribution_partial)
    )
    arrived, arrived_target = (
        lax.all_to_all(partial_buffer, BAND_SUB, split_axis=0, concat_axis=0, tiled=True),
        lax.all_to_all(target_buffer, BAND_SUB, split_axis=0, concat_axis=0, tiled=True),
    )
    selector = (arrived_target[None, :] == jnp.arange(TB_DEV, dtype=jnp.int32)[:, None]).astype(
        jnp.float32
    )
    sums = jnp.dot(
        selector,
        arrived.reshape(positions, (field_count + 1) * block_cells),
        precision=lax.Precision.HIGHEST,
    )
    sums = sums.reshape(TB_DEV, field_count + 1, block_cells)
    numer = sums[:, :field_count, :]
    fraction = sums[:, field_count, :]
    filled = numer + jnp.maximum(0.25 - fraction, 0.0)[:, None, :] * land_mean[None, :, None]
    remap_output = filled / jnp.maximum(fraction, 0.25)[:, None, :]
    return remap_output.transpose(1, 0, 2).reshape(field_count, TB_DEV * block_cells)


def solution(mesh):
    finer = Mesh(
        mesh.devices.reshape(4, 4, 2, mesh.shape["sub"]), ("band_0", "band_1", "band_2", "sub")
    )
    return jax.shard_map(
        body,
        mesh=finer,
        in_specs=(
            P(None, BAND_SUB),
            P(BAND_SUB),
            P(BAND_SUB, None, None),
            P(BAND_SUB),
            P(BAND_SUB),
            P(BAND_SUB),
        ),
        out_specs=P(None, BAND_SUB),
        check_vma=False,
    )
```

profile of v0, /device:TPU:0, one launch (start us, length us, event | category | flops | bytes accessed | tf_op | source)
XLA Modules:
  0.0 143.6 jit_solution(13160390631848578541)
XLA Ops:
  0.0 0.0 copy-start.1
  0.0 0.7 compare_select_fusion
  0.7 1.6 %scatter_custom_fusion = s32[512]{0:T(512)S(1)} fusion(s32[256]{0:T(256)S(1)} %compare_select_fusion, s32[256]{0:T(256)} %param.10, s32[]{:T(128)} %constant.5.clone.1), kind=kCustom, calls=%fused_computation.28 | custom fusion | bytes 2560 | tf_op jit(solution)/shard_map/scatter | solution.py:36
  2.3 0.7 all_to_all.9
  3.0 11.2 %all-to-all-start = ((s32[128,4,1]{1,2,0:T(1,128)}), s32[128,4,1]{1,2,0:T(1,128)S(1)}, u32[]{:S(2)}, u32[]{:S(2)}) async-start(s32[128,4,1]{1,2,0:T(1,128)} %bitcast), calls=%async_computation | async-start | bytes 131072 | tf_op jit(solution)/shard_map/all_to_all | solution.py:47
  14.9 1.4 copy.14
  16.3 0.1 slice.10
  16.3 0.0 copy-done.1
  16.3 0.1 fusion.9
  16.4 0.3 multiply_convert_fusion.1
  16.8 0.5 fusion.6
  17.3 4.7 %fusion.2 = f32[256,13,128]{2,1,0:T(8,128)S(1)} fusion(bf16[256,128,128]{2,1,0:T(8,128)(2,1)} %param.8, bf16[256,1,128]{2,1,0:T(2,128)(2,1)S(1)} %multiply_convert_fusion.1, bf16[256,12,128]{2,1,0:T(8,128)(2,1)S(1)} %fusion.6), kind=kOutput, calls=%fused_computation.5 | convolution fusion | flops 110755840 | bytes 10944512 | tf_op jit(solution)/shard_map/myr,mrw->myw/dot_general | solution.py:37
  21.9 2.3 %broadcast_in_dim.8 = f32[512,13,128]{2,1,0:T(8,128)} broadcast(f32[]{:T(128)} %constant.7.clone.1), dimensions={} | broadcast | bytes 3407876 | tf_op jit(solution)/shard_map/broadcast_in_dim | solution.py:41
  24.2 26.5 %scatter_fusion = f32[512,13,128]{2,1,0:T(8,128)} fusion(f32[512,13,128]{2,1,0:T(8,128)} %broadcast_in_dim.8, s32[256]{0:T(256)S(1)} %compare_select_fusion, f32[256,13,128]{2,1,0:T(8,128)S(1)} %fusion.2), kind=kCustom, calls=%fused_computation.1 | custom fusion | bytes 5112832 | tf_op jit(solution)/shard_map/scatter | solution.py:43
  50.7 0.0 copy-start
  50.7 0.0 all-to-all-done
  50.7 10.3 %all-to-all-start.1 = ((f32[512,13,128]{2,1,0:T(8,128)}), f32[512,13,128]{2,1,0:T(8,128)}, u32[]{:S(2)}, u32[]{:S(2)}) async-start(f32[512,13,128]{2,1,0:T(8,128)} %scatter_fusion), calls=%async_computation.1 | async-start | bytes 8388608 | tf_op jit(solution)/shard_map/all_to_all | solution.py:46
  61.0 0.3 mul.65
  61.3 0.0 copy-done
  61.4 0.4 convert_reduce_fusion
  61.7 0.7 fusion.8
  62.4 47.0 %all-reduce.2 = (f32[12]{0:T(128)S(1)}, f32[]{:T(128)}) all-reduce(f32[12]{0:T(128)S(1)} %convert_reduce_fusion, f32[]{:T(128)} %fusion.8), channel_id=1, replica_groups=mesh['band_0'=4,'band_1'=4,'band_2'=2,'sub'=4] {'band_0'}, use_global_device_ids=true, to_apply=%region_3.0 | all-reduce | flops 13 | bytes 104 | tf_op jit(solution)/shard_map/psum | solution.py:14
  109.4 11.5 %all-reduce.1 = (f32[12]{0:T(128)S(1)}, f32[]{:T(128)}) all-reduce(f32[12]{0:T(128)S(1)} %get-tuple-element.9, f32[]{:T(128)} %get-tuple-element.10), channel_id=1, replica_groups=mesh['band_0'=4,'band_1'=4,'band_2'=2,'sub'=4] {'band_1'}, use_global_device_ids=true, to_apply=%region_4.0 | all-reduce | flops 13 | bytes 104 | tf_op jit(solution)/shard_map/psum | solution.py:14
  120.9 3.1 %all-reduce.3 = (f32[12]{0:T(128)S(1)}, f32[]{:T(128)}) all-reduce(f32[12]{0:T(128)S(1)} %get-tuple-element.7, f32[]{:T(128)} %get-tuple-element.8), channel_id=1, replica_groups=mesh['band_0'=4,'band_1'=4,'band_2'=2,'sub'=4] {'band_2'}, use_global_device_ids=true, to_apply=%region_5.0 | all-reduce | flops 13 | bytes 104 | tf_op jit(solution)/shard_map/psum | solution.py:14
  124.0 11.6 %all-reduce = (f32[12]{0:T(128)S(1)}, f32[]{:T(128)}) all-reduce(f32[12]{0:T(128)S(1)} %get-tuple-element.11, f32[]{:T(128)} %get-tuple-element.12), channel_id=1, replica_groups=mesh['band_0'=4,'band_1'=4,'band_2'=2,'sub'=4] {'sub'}, use_global_device_ids=true, to_apply=%region_6.0 | all-reduce | flops 13 | bytes 104 | tf_op jit(solution)/shard_map/psum | solution.py:14
  136.2 0.5 broadcast.54
  136.7 0.8 reduce.5
  137.5 0.1 eq.15
  137.7 0.0 all-to-all-done.1
  137.7 3.5 %copy.13 = f32[512,13,128]{0,2,1:T(8,128)S(1)} copy(f32[512,13,128]{2,1,0:T(8,128)} %all-to-all-done.1) | data formatting | bytes 6815744 | tf_op jit(solution)/shard_map/all_to_all | solution.py:46
  141.2 1.6 %fusion = f32[16,13,128]{2,0,1:T(8,128)S(1)} fusion(f32[512,13,128]{0,2,1:T(8,128)S(1)} %copy.13, s32[512]{0:T(512)S(1)} %eq.15), kind=kOutput, calls=%fused_computation.2 | convolution fusion | flops 163586048 | bytes 3516416 | tf_op jit(solution)/shard_map/dot_general | solution.py:52
  142.8 0.1 fusion.11
  142.9 0.7 copy.15
  (5 shorter events, 0.0 us)
Async XLA Ops:
  0.0 16.3 %copy-start.1 = (s32[32768]{0:T(1024)S(1)}, s32[32768]{0:T(1024)}, u32[]{:S(2)}) copy-start(s32[32768]{0:T(1024)} %param.7) | copy-start | bytes 393220
  3.0 47.7 %all-to-all-start = ((s32[128,4,1]{1,2,0:T(1,128)}), s32[128,4,1]{1,2,0:T(1,128)S(1)}, u32[]{:S(2)}, u32[]{:S(2)}) async-start(s32[128,4,1]{1,2,0:T(1,128)} %bitcast), calls=%async_computation | async-start | bytes 131072 | tf_op jit(solution)/shard_map/all_to_all | solution.py:47
  50.7 10.7 %copy-start = (bf16[12,32768]{1,0:T(8,128)(2,1)S(1)}, bf16[12,32768]{1,0:T(8,128)(2,1)}, u32[]{:S(2)}) copy-start(bf16[12,32768]{1,0:T(8,128)(2,1)} %param.6) | copy-start | bytes 2359300
  50.7 87.0 %all-to-all-start.1 = ((f32[512,13,128]{2,1,0:T(8,128)}), f32[512,13,128]{2,1,0:T(8,128)}, u32[]{:S(2)}, u32[]{:S(2)}) async-start(f32[512,13,128]{2,1,0:T(8,128)} %scatter_fusion), calls=%async_computation.1 | async-start | bytes 8388608 | tf_op jit(solution)/shard_map/all_to_all | solution.py:46
where the time goes:
time: 145 us; the launch traced here: 144 us
  blocking collectives  73.1 us (50%)
  local copies, waits for them, and re-layouts  37.7 us (26%)
  starting transfers between devices  21.5 us (15%)
  matrix products  6.3 us (4%)
  other arithmetic  3.65 us (3%)
  between operations  1.46 us (1%)
    psum x4, blocking collectives, one_axis_at_a_time(): return functools.reduce(lax.psum, axes, array)  73.1 us
    scatter x1, local copies, waits for them, and re-layouts, body(): partial_buffer = jnp.zeros((positions, field_count + 1, block_cells), jnp...  26.5 us
    all_to_all x1, starting transfers between devices, body(): lax.all_to_all(target_buffer, BAND_SUB, split_axis=0, concat_axis=0, tile...  11.2 us
    all_to_all x1, starting transfers between devices, body(): lax.all_to_all(partial_buffer, BAND_SUB, split_axis=0, concat_axis=0, til...  10.3 us
    dot_general x1, matrix products, body(): jnp.einsum('myr,mrw->myw', stacked_fields, intersection, preferred_elemen...  4.67 us
    all_to_all x1, local copies, waits for them, and re-layouts, body(): lax.all_to_all(partial_buffer, BAND_SUB, split_axis=0, concat_axis=0, til...  3.51 us
  transfers between devices with their start and end apart: 2, of which 0 were waited for; matrix products, arithmetic and copies ran while one was open for 27% of the time, Pallas kernels for 0%

commit v1 on v0

v1 whole, which is shorter than its diff:
```python
import functools

import jax
import jax.numpy as jnp
from jax import lax
from jax.experimental import pallas as pl
from jax.experimental.pallas import tpu as pltpu
from jax.sharding import PartitionSpec as P

CELL = 128
BLOCKS = 256
STEP = 32
TARGETS = 16
CHUNK = 64
ROWS = (4, 4, 5)
FIRST = (0, 4, 8)
ORDER = ("zxy", "xyz", "yzx")
MESH = pl.DeviceIdType.MESH


def local_kernel(
    pos_ref, target_ref, live_ref, fields_ref, mask_ref, weights_ref,
    out_a, out_b, out_c, codes_ref, total_ref, code_a, code_b, code_c,
):
    step = pl.program_id(0)
    outs = (out_a, out_b, out_c)
    codes = (code_a, code_b, code_c)

    @pl.when(step == 0)
    def _():
        total_ref[...] = jnp.zeros_like(total_ref)
        for ref in outs + codes:
            rows = ref.shape[0] // 8

            @pl.loop(0, rows // 8)
            def _(i):
                ref[pl.ds(pl.multiple_of(i * 64, 64), 64), :] = jnp.zeros((64, CELL), ref.dtype)

    total = total_ref[...]
    for block in range(STEP):
        index = step * STEP + block
        live = (index < live_ref[0]).astype(jnp.int32)
        mask = (mask_ref[pl.ds(block, 1), :] * live).astype(jnp.float32)
        values = fields_ref[:, block * CELL : (block + 1) * CELL].astype(jnp.float32)
        stacked = jnp.concatenate([values * mask, jnp.broadcast_to(mask, (4, CELL))], axis=0)
        total += stacked
        contrib = jnp.dot(
            stacked.astype(jnp.bfloat16), weights_ref[block], preferred_element_type=jnp.float32
        )
        target = target_ref[index]
        for g in range(3):
            pos = pos_ref[g, index]
            part = pos // CHUNK
            inner = pos - part * CHUNK
            base = part * (ROWS[g] * CHUNK) + inner
            outs[g][pl.ds(base, ROWS[g], stride=CHUNK), :] = contrib[FIRST[g] : FIRST[g] + ROWS[g]]
            code = (inner // 4) * TARGETS + target
            codes[g][pl.ds(pos, 1), :] = jnp.full((1, CELL), code.astype(jnp.float32))
    total_ref[...] = total

    @pl.when(step == BLOCKS // STEP - 1)
    def _():
        low = lax.broadcasted_iota(jnp.int32, (8, CELL), 1) < CHUNK
        for g in range(3):
            for pair in range(4):
                turned = codes[g][pl.ds(pair * CELL, CELL), :].T[0:8]
                rolled = pltpu.roll(turned, CHUNK, 1)
                even = jnp.where(low, turned, rolled).astype(jnp.int32)
                odd = jnp.where(low, rolled, turned).astype(jnp.int32)
                codes_ref[g, 2 * pair] = even
                codes_ref[g, 2 * pair + 1] = odd


def exchange_kernel(
    in_a, in_b, in_c, codes_ref, total_ref, out_ref,
    r1_a, r1_b, r1_c, c1, s2_a, s2_b, s2_c, r2_a, r2_b, r2_c,
    s3_a, s3_b, s3_c, r3_a, r3_b, r3_c, final_ref,
    t_send, t1, t2, t3,
    send1, recv1, csend, crecv, own1, send2, recv2, send3, recv3, tsend, trecv,
):
    ins = (in_a, in_b, in_c)
    r1 = (r1_a, r1_b, r1_c)
    s2 = (s2_a, s2_b, s2_c)
    r2 = (r2_a, r2_b, r2_c)
    s3 = (s3_a, s3_b, s3_c)
    r3 = (r3_a, r3_b, r3_c)
    band = lax.axis_index("band")
    here = {
        "y": band // 8,
        "x": lax.rem(band // 2, 4),
        "c": lax.rem(band, 2),
        "z": lax.axis_index("sub"),
    }

    def peer(dim, shift, core=0):
        at = dict(here)
        at[dim] = lax.rem(here[dim] + shift, 4)
        at["c"] = lax.rem(here["c"] + core, 2)
        return at, ((at["y"] * 4 + at["x"]) * 2 + at["c"], at["z"])

    def remote(src, dst, send, recv, device):
        return pltpu.make_async_remote_copy(
            src_ref=src, dst_ref=dst, send_sem=send, recv_sem=recv,
            device_id=device, device_id_type=MESH,
        )

    barrier = pltpu.get_barrier_semaphore()
    count = 0
    for dim in "zxy":
        for shift in (1, 2, 3):
            for core in (0, 1):
                pl.semaphore_signal(
                    barrier, inc=1, device_id=peer(dim, shift, core)[1], device_id_type=MESH
                )
                count += 1
    pl.semaphore_signal(barrier, inc=1, device_id=peer("z", 0, 1)[1], device_id_type=MESH)
    pl.semaphore_wait(barrier, count + 1)

    sends = []
    first = [[None] * 8 for _ in range(3)]
    first_codes = [[None] * 8 for _ in range(3)]
    totals_first = []
    local = []
    for shift, core in ((2, 0), (2, 1), (1, 0), (3, 0), (1, 1), (3, 1), (0, 1)):
        for g in range(3):
            dim = ORDER[g][0]
            at, device = peer(dim, shift, core)
            slot = shift * 2 + core
            code = remote(
                codes_ref.at[g, at["c"] * 4 + at[dim]], c1.at[g, slot],
                csend.at[g, slot], crecv.at[g, slot], device,
            )
            code.start()
            copy = remote(
                ins[g].at[at["c"] * 4 + at[dim]], r1[g].at[slot],
                send1.at[g, slot], recv1.at[g, slot], device,
            )
            copy.start()
            sends += [code, copy]
            first[g][slot] = copy
            first_codes[g][slot] = code
            if g == 0:
                whole = remote(total_ref, t1.at[slot], tsend.at[0, slot], trecv.at[0, slot], device)
                whole.start()
                sends.append(whole)
                totals_first.append((slot, whole))
    for g in range(3):
        mine = here["c"] * 4 + here[ORDER[g][0]]
        copy = pltpu.make_async_copy(ins[g].at[mine], r1[g].at[0], own1.at[g])
        copy.start()
        local.append(copy)
    total = total_ref[...]
    for slot, copy in totals_first:
        copy.wait_recv()
        total += t1[slot]
    t_send[0] = total
    totals_second = []
    for shift in (1, 2, 3):
        copy = remote(
            t_send.at[0], t2.at[shift - 1], tsend.at[1, shift], trecv.at[1, shift],
            peer("x", shift)[1],
        )
        copy.start()
        sends.append(copy)
        totals_second.append(copy)

    second = []
    for g in range(3):
        mine = here["c"] * 4 + here[ORDER[g][0]]
        low = lax.broadcasted_iota(jnp.int32, (1, CELL), 1) < CHUNK
        lanes = []
        for pair in range(4):
            if pair == 0:
                left = codes_ref[g, mine]
            else:
                first_codes[g][2 * pair].wait_recv()
                left = c1[g, 2 * pair]
            first_codes[g][2 * pair + 1].wait_recv()
            right = c1[g, 2 * pair + 1]
            lanes.append(jnp.where(low, left[0:1], right[0:1]))
        wide = jnp.concatenate(lanes, axis=1)
        rows = lax.broadcasted_iota(jnp.int32, (256, 512), 0)
        select = jnp.where(rows == wide, 1.0, 0.0).astype(jnp.bfloat16)
        local[g].wait()
        for slot in range(1, 8):
            first[g][slot].wait_recv()
        for row in range(ROWS[g]):
            data = jnp.concatenate([r1[g][slot, row] for slot in range(8)], axis=0)
            high = data.astype(jnp.bfloat16)
            rest = (data - high.astype(jnp.float32)).astype(jnp.bfloat16)
            both = jnp.dot(
                select, jnp.concatenate([high, rest], axis=1), preferred_element_type=jnp.float32
            )
            summed = both[:, :CELL] + both[:, CELL:]
            for part in range(4):
                s2[g][part, row] = summed[part * 64 : (part + 1) * 64]
        dim = ORDER[g][1]
        copies = []
        for shift in (2, 1, 3):
            at, device = peer(dim, shift)
            copy = remote(
                s2[g].at[at[dim]], r2[g].at[shift - 1], send2.at[g, shift], recv2.at[g, shift], device
            )
            copy.start()
            sends.append(copy)
            copies.append(copy)
        second.append(copies)

    total = t_send[0]
    for shift in (1, 2, 3):
        totals_second[shift - 1].wait_recv()
        total += t2[shift - 1]
    t_send[1] = total
    totals_third = []
    for shift in (1, 2, 3):
        copy = remote(
            t_send.at[1], t3.at[shift - 1], tsend.at[2, shift], trecv.at[2, shift],
            peer("y", shift)[1],
        )
        copy.start()
        sends.append(copy)
        totals_third.append(copy)

    third = []
    for g in range(3):
        for copy in second[g]:
            copy.wait_recv()
        mine = here[ORDER[g][1]]
        for row in range(ROWS[g]):
            summed = s2[g][mine, row] + r2[g][0, row] + r2[g][1, row] + r2[g][2, row]
            for part in range(4):
                s3[g][part, row] = summed[part * TARGETS : (part + 1) * TARGETS]
        dim = ORDER[g][2]
        copies = []
        for shift in (2, 1, 3):
            at, device = peer(dim, shift)
            copy = remote(
                s3[g].at[at[dim]], r3[g].at[shift - 1], send3.at[g, shift], recv3.at[g, shift], device
            )
            copy.start()
            sends.append(copy)
            copies.append(copy)
        third.append(copies)

    total = t_send[1]
    for shift in (1, 2, 3):
        totals_third[shift - 1].wait_recv()
        total += t3[shift - 1]
    total = jnp.sum(total, axis=1, keepdims=True)
    mean = total[0:12] / jnp.maximum(total[12:13], 1.0)
    for g in range(3):
        for copy in third[g]:
            copy.wait_recv()
        mine = here[ORDER[g][2]]
        for row in range(ROWS[g]):
            summed = s3[g][mine, row] + r3[g][0, row] + r3[g][1, row] + r3[g][2, row]
            final_ref[pl.ds((FIRST[g] + row) * TARGETS, TARGETS), :] = summed
    for t in range(TARGETS):
        numer = final_ref[pl.ds(t, 12, stride=TARGETS), :]
        fraction = final_ref[pl.ds(12 * TARGETS + t, 1), :]
        filled = numer + jnp.maximum(0.25 - fraction, 0.0) * mean
        out_ref[:, t * CELL : (t + 1) * CELL] = filled / jnp.maximum(fraction, 0.25)
    for copy in sends:
        copy.wait_send()


def body(fields, land_mask, intersection, send_slot, target_block, live_blocks):
    k = send_slot % 4
    owner = send_slot // 4
    z = owner % 4
    c = (owner // 4) % 2
    x = (owner // 8) % 4
    y = owner // 32
    at = {"x": x, "y": y, "z": z}
    pos = jnp.stack(
        [
            ((((c * 4 + at[o[0]]) * 4 + at[o[1]]) * 4 + at[o[2]]) * 4 + k).astype(jnp.int32)
            for o in ORDER
        ]
    )
    smem = pl.BlockSpec(memory_space=pltpu.SMEM)
    f32 = jnp.float32
    sizes = [8 * r * CHUNK for r in ROWS]
    whole = lambda shape: pl.BlockSpec(shape, lambda i: (0,) * len(shape))
    *parts, codes, total = pl.pallas_call(
        local_kernel,
        grid=(BLOCKS // STEP,),
        in_specs=[
            smem, smem, smem,
            pl.BlockSpec((12, STEP * CELL), lambda i: (0, i)),
            pl.BlockSpec((STEP, CELL), lambda i: (i, 0)),
            pl.BlockSpec((STEP, CELL, CELL), lambda i: (i, 0, 0)),
        ],
        out_specs=[whole((n, CELL)) for n in sizes] + [whole((3, 8, 8, CELL)), whole((16, CELL))],
        out_shape=[jax.ShapeDtypeStruct((n, CELL), f32) for n in sizes]
        + [jax.ShapeDtypeStruct((3, 8, 8, CELL), jnp.int32), jax.ShapeDtypeStruct((16, CELL), f32)],
        scratch_shapes=[pltpu.VMEM((512, CELL), f32)] * 3,
        compiler_params=pltpu.CompilerParams(dimension_semantics=("arbitrary",)),
        name="local",
    )(pos, target_block, live_blocks, fields, land_mask.reshape(BLOCKS, CELL), intersection)
    parts = [p.reshape(8, r, CHUNK, CELL) for p, r in zip(parts, ROWS)]
    vmem = pl.BlockSpec(memory_space=pltpu.VMEM)
    hbm = pl.BlockSpec(memory_space=pl.ANY)
    dma = pltpu.SemaphoreType.DMA
    return pl.pallas_call(
        exchange_kernel,
        in_specs=[hbm, hbm, hbm, vmem, vmem],
        out_specs=vmem,
        out_shape=jax.ShapeDtypeStruct((12, TARGETS * CELL), f32),
        scratch_shapes=[pltpu.VMEM((8, r, CHUNK, CELL), f32) for r in ROWS]
        + [pltpu.VMEM((3, 8, 8, CELL), jnp.int32)]
        + [pltpu.VMEM((4, r, CHUNK, CELL), f32) for r in ROWS]
        + [pltpu.VMEM((3, r, CHUNK, CELL), f32) for r in ROWS]
        + [pltpu.VMEM((4, r, TARGETS, CELL), f32) for r in ROWS]
        + [pltpu.VMEM((3, r, TARGETS, CELL), f32) for r in ROWS]
        + [pltpu.VMEM((13 * TARGETS, CELL), f32)]
        + [pltpu.VMEM((2, 16, CELL), f32), pltpu.VMEM((8, 16, CELL), f32)]
        + [pltpu.VMEM((3, 16, CELL), f32), pltpu.VMEM((3, 16, CELL), f32)]
        + [dma((3, 8)), dma((3, 8)), dma((3, 8)), dma((3, 8)), dma((3,))]
        + [dma((3, 4)), dma((3, 4)), dma((3, 4)), dma((3, 4)), dma((3, 8)), dma((3, 8))],
        compiler_params=pltpu.CompilerParams(collective_id=0, has_side_effects=True),
        name="exchange",
    )(*parts, codes, total)


def solution(mesh):
    axes = ("band", "sub")
    return jax.shard_map(
        body,
        mesh=mesh,
        in_specs=(P(None, axes), P(axes), P(axes, None, None), P(axes), P(axes), P(axes)),
        out_specs=P(None, axes),
        check_vma=False,
    )
```

time: 145 us -> 61 us (0.42)
  blocking collectives: 73.1 us -> 0 us
  Pallas kernels: 0 us -> 56.4 us
  local copies, waits for them, and re-layouts: 37.7 us -> 1.57 us
  starting transfers between devices: 21.5 us -> 0 us
  matrix products: 6.3 us -> 0 us
  other arithmetic: 3.65 us -> 2.01 us
    psum x4 -> x0, blocking collectives: 73.1 us -> none  [one_axis_at_a_time(): return functools.reduce(lax.psum, axes, array)]
    pallas_call x0 -> x2, Pallas kernels: none -> 56.4 us  [the longest x1 41.4 us: body(): pl.pallas_call(exchange_kernel, in_specs=[hbm, hbm, hbm, vmem, vmem], out...]
    scatter x2 -> x0, local copies, waits for them, and re-layouts: 28 us -> none  [the longest x1 26.5 us: body(): partial_buffer = jnp.zeros((positions, field_count + 1, block_cells), jnp...]
    all_to_all x2 -> x0, starting transfers between devices: 21.5 us -> none  [the longest x1 11.2 us: body(): lax.all_to_all(target_buffer, BAND_SUB, split_axis=0, concat_axis=0, tile...]
    dot_general x2 -> x0, matrix products: 6.3 us -> none  [the longest x1 4.67 us: body(): jnp.einsum('myr,mrw->myw', stacked_fields, intersection, preferred_elemen...]
    all_to_all x3 -> x0, local copies, waits for them, and re-layouts: 4.76 us -> none  [the longest x1 3.51 us: body(): lax.all_to_all(partial_buffer, BAND_SUB, split_axis=0, concat_axis=0, til...]
    broadcast_in_dim x1 -> x0, local copies, waits for them, and re-layouts: 2.26 us -> none  [body(): jnp.zeros((positions, field_count + 1, block_cells), jnp.float32)]
  transfers between devices with their start and end apart: 2 -> 0, of which waited for: 0 -> 0; matrix products, arithmetic and copies ran while one was open for 27% -> 0% of each run, Pallas kernels for 0% -> 0%
where the time goes in v1:
time: 61 us; the launch traced here: 60.7 us
  Pallas kernels  56.4 us (92%)
  other arithmetic  2.01 us (3%)
  local copies, waits for them, and re-layouts  1.57 us (3%)
  between operations  0.66 us (1%)
    pallas_call x1, Pallas kernels, body(): pl.pallas_call(exchange_kernel, in_specs=[hbm, hbm, hbm, vmem, vmem], out...  41.4 us
    pallas_call x1, Pallas kernels, body(): pl.pallas_call(local_kernel, grid=(BLOCKS // STEP,), in_specs=[smem, smem...  15 us
    unnamed x1, local copies, waits for them, and re-layouts  1.57 us
    add x2, other arithmetic, body(): (((c * 4 + at[o[0]]) * 4 + at[o[1]]) * 4 + at[o[2]]) * 4 + k  1.41 us

profile of v1, /device:TPU:0, one launch (start us, length us, event | category | flops | bytes accessed | tf_op | source)
XLA Modules:
  0.0 60.7 jit_solution(17463788272707633540)
XLA Ops:
  0.7 0.7 %multiply_add_fusion.2 = (s32[256]{0:T(256)S(1)}, s32[256]{0:T(256)S(1)}, s32[256]{0:T(256)S(1)}, s32[256]{0:T(256)S(1)}) fusion(s32[256]{0:T(256)} %param.9), kind=kLoop, calls=%fused_computation.28 | loop fusion | flops 22528 | bytes 5120 | tf_op jit(solution)/shard_map/add | solution.py:277
  1.4 0.7 %multiply_add_fusion.1 = (s32[256]{0:T(256)S(1)}, s32[256]{0:T(256)S(1)}) fusion(s32[256]{0:T(256)S(1)} %get-tuple-element.16, s32[256]{0:T(256)S(1)} %get-tuple-element.17, s32[256]{0:T(256)S(1)} %get-tuple-element.18, s32[256]{0:T(256)} %param.9), kind=kLoop, calls=%fused_computation.27 | loop fusion | flops 12288 | bytes 6144 | tf_op jit(solution)/shard_map/add | solution.py:277
  2.1 0.6 pad_add_fusion.pos_ref
  2.7 15.0 %local.1 = (f32[2048,128]{1,0:T(8,128)}, f32[2048,128]{1,0:T(8,128)}, f32[2560,128]{1,0:T(8,128)}, s32[3,8,8,128]{3,2,1,0:T(8,128)}, f32[16,128]{1,0:T(8,128)}) custom-call(s32[3,256]{1,0:T(4,128)} %pad_add_fusion.pos_ref, s32[256]{0:T(256)} %target_ref.1, s32[1]{0:T(128)S(6)} %copy.8.live_ref, bf16[12,32768]{1,0:T(8,128)(2,1)} %fields_ref.1, ...), custom_call_target="tpu_custom_call" | custom-call | tf_op jit(solution)/shard_map/local/pallas_call | solution.py:285
  17.7 41.4 %exchange.1 = f32[12,2048]{1,0:T(8,128)} custom-call(f32[8,4,64,128]{3,2,1,0:T(8,128)} %bitcast.8, f32[8,4,64,128]{3,2,1,0:T(8,128)} %bitcast.9, f32[8,5,64,128]{3,2,1,0:T(8,128)} %bitcast.7, s32[3,8,8,128]{3,2,1,0:T(8,128)} %get-tuple-element.13.codes_ref, f32[16,128]{1,0:T(8,128)} %get-tuple-element.14.total_ref), custom_call_target="tpu_custom_call" | custom-call | tf_op jit(solution)/shard_map/exchange/pallas_call | solution.py:305
  59.1 1.6 %copy.9 = f32[12,2048]{1,0:T(8,128)} copy(f32[12,2048]{1,0:T(8,128)} %exchange.1) | data formatting | bytes 196608

commit v2 on v1

v2 whole, which is shorter than its diff:
```python
import jax
import jax.numpy as jnp
from jax import lax
from jax.experimental import pallas as pl
from jax.experimental.pallas import tpu as pltpu
from jax.sharding import PartitionSpec as P

CELL = 128
BLOCKS = 256
TARGETS = 16
CHUNK = 64
ROWS = (4, 4, 5)
FIRST = (0, 4, 8)
STAGES = ("zxy", "xyz", "yzx")
SLOTS = ("zxy", "xzy", "yzx")
MESH = pl.DeviceIdType.MESH
F32 = jnp.float32
BF16 = jnp.bfloat16
WEIGHT_COPIES = 4


def encode(tiles, lane, write):
    top = jnp.abs(tiles[0])
    for tile in tiles[1:]:
        top = jnp.maximum(top, jnp.abs(tile))
    top = jnp.maximum(jnp.max(top, axis=1, keepdims=True), 1e-25)
    power = jnp.ceil(jnp.log2(top) + 0.02)
    down = jnp.exp2(-power)
    for row, tile in enumerate(tiles):
        small = tile * down
        code = small * lax.rsqrt(jnp.abs(small) + 1e-30) * 32768.0
        write(row, jnp.round(code).astype(jnp.int32).astype(jnp.int16))
    scale = jnp.exp2(power - 30.0)
    lanes = lax.broadcasted_iota(jnp.int32, (16, CELL), 1) % CHUNK
    slots = lax.broadcasted_iota(jnp.int32, (16, CELL), 0) + lane
    return jnp.sum(jnp.where(lanes == slots, scale, 0.0), axis=0, keepdims=True)


def decode(codes):
    value = codes.astype(F32)
    value = value * jnp.abs(value)
    high = value.astype(BF16)
    return jnp.concatenate([high, (value - high.astype(F32)).astype(BF16)], axis=1)


def kernel(
    live_ref, slot_hbm, target_hbm, fields_hbm, mask_hbm, weights_hbm, out_ref,
    slot_ref, target_ref, fields_ref, mask_ref, weights_ref, stack_ref, index_vmem, index_smem,
    st_a, st_b, st_c, q_a, q_b, q_c, r1_a, r1_b, r1_c, cs, c1,
    s2_a, s2_b, s2_c, q2_a, q2_b, q2_c, r2_a, r2_b, r2_c, cs2, c2,
    s3_a, s3_b, s3_c, r3_a, r3_b, r3_c, final_ref, t_send, t1, t2, t3,
    load, wload, send1, recv1, csend, crecv, send2, recv2, c2send, c2recv, send3, recv3, tsend, trecv,
):
    stage = (st_a, st_b, st_c)
    q = (q_a, q_b, q_c)
    r1 = (r1_a, r1_b, r1_c)
    s2 = (s2_a, s2_b, s2_c)
    q2 = (q2_a, q2_b, q2_c)
    r2 = (r2_a, r2_b, r2_c)
    s3 = (s3_a, s3_b, s3_c)
    r3 = (r3_a, r3_b, r3_c)
    band = lax.axis_index("band")
    here = {
        "y": band // 8,
        "x": lax.rem(band // 2, 4),
        "c": lax.rem(band, 2),
        "z": lax.axis_index("sub"),
    }

    def peer(dim, shift, core=0):
        at = dict(here)
        at[dim] = lax.rem(here[dim] + shift, 4)
        at["c"] = lax.rem(here["c"] + core, 2)
        return at, ((at["y"] * 4 + at["x"]) * 2 + at["c"], at["z"])

    def remote(src, dst, send, recv, device):
        return pltpu.make_async_remote_copy(
            src_ref=src, dst_ref=dst, send_sem=send, recv_sem=recv,
            device_id=device, device_id_type=MESH,
        )

    loads = [
        pltpu.make_async_copy(slot_hbm, slot_ref, load.at[0]),
        pltpu.make_async_copy(target_hbm, target_ref, load.at[1]),
        pltpu.make_async_copy(mask_hbm, mask_ref, load.at[2]),
        pltpu.make_async_copy(fields_hbm, fields_ref, load.at[3]),
    ]
    size = BLOCKS // WEIGHT_COPIES
    weight_loads = [
        pltpu.make_async_copy(
            weights_hbm.at[pl.ds(i * size, size)], weights_ref.at[pl.ds(i * size, size)], wload.at[i]
        )
        for i in range(WEIGHT_COPIES)
    ]
    for copy in loads + weight_loads:
        copy.start()

    barrier = pltpu.get_barrier_semaphore()
    count = 0
    for dim in "zxy":
        for shift in (1, 2, 3):
            for core in (0, 1):
                pl.semaphore_signal(
                    barrier, inc=1, device_id=peer(dim, shift, core)[1], device_id_type=MESH
                )
                count += 1
    pl.semaphore_signal(barrier, inc=1, device_id=peer("z", 0, 1)[1], device_id_type=MESH)

    loads[0].wait()
    loads[1].wait()
    low = lax.broadcasted_iota(jnp.int32, (1, CELL), 1) < CHUNK
    blocks = lax.broadcasted_iota(jnp.int32, (8, BLOCKS), 1)
    kind = lax.broadcasted_iota(jnp.int32, (8, BLOCKS), 0)
    facts = jnp.where(kind == 0, blocks - BLOCKS, jnp.broadcast_to(target_ref[...], (8, BLOCKS)))
    facts = facts.astype(F32).astype(BF16)
    place = lax.broadcasted_iota(jnp.int32, (512, 1), 0)
    along = lax.broadcasted_iota(jnp.int32, (1, 512), 1)
    cs[...] = jnp.zeros_like(cs)
    for g in range(3):
        order = SLOTS[g]

        def split(n):
            chunk, second, third, k = n // 64, (n // 16) % 4, (n // 4) % 4, n % 4
            if g > 0:
                second = second + 1
            at = {
                order[0]: (here[order[0]] + chunk // 2) % 4,
                order[1]: (here[order[1]] + second) % 4,
                order[2]: (here[order[2]] + third) % 4,
                "c": (here["c"] + chunk) % 2,
            }
            return at, k

        at, k = split(place)
        wanted = (((at["y"] * 4 + at["x"]) * 2 + at["c"]) * 4 + at["z"]) * 4 + k
        hits = jnp.where(wanted == slot_ref[...], 1.0, 0.0).astype(BF16)
        found = lax.dot_general(
            facts, hits, (((1,), (1,)), ((), ())), preferred_element_type=F32
        )
        if g == 0:
            index_vmem[...] = (found[0:1] + BLOCKS).astype(jnp.int32)
            index_copy = pltpu.make_async_copy(index_vmem, index_smem, load.at[4])
            index_copy.start()
        at, k = split(along)
        owner = at[STAGES[g][1]] * 4 + at[STAGES[g][2]]
        code = found[1:2] + (owner * TARGETS).astype(F32)
        for pair in range(4):
            both = code[:, pair * CELL : (pair + 1) * CELL]
            rolled = pltpu.roll(both, CHUNK, 1)
            cs[g, 2 * pair, 0:1, :] = jnp.where(low, both, rolled)
            cs[g, 2 * pair + 1, 0:1, :] = jnp.where(low, rolled, both)

    loads[2].wait()
    loads[3].wait()
    live = live_ref[0]

    def build(i, total):
        for j in range(8):
            block = i * 8 + j
            alive = (block < live).astype(jnp.int32)
            mask = (mask_ref[pl.ds(block, 1), :] * alive).astype(F32)
            values = fields_ref[:, pl.ds(pl.multiple_of(block * CELL, CELL), CELL)].astype(F32)
            stacked = jnp.concatenate([values * mask, jnp.broadcast_to(mask, (4, CELL))], axis=0)
            total += stacked
            stack_ref[block] = stacked.astype(BF16)
        return total

    total = lax.fori_loop(0, BLOCKS // 8, build, jnp.zeros((16, CELL), F32))
    stack_ref[BLOCKS] = jnp.zeros((16, CELL), BF16)
    t_send[0] = total
    pl.semaphore_wait(barrier, count + 1)

    sends = []
    totals_first = []
    for slot in range(1, 8):
        copy = remote(
            t_send.at[0], t1.at[slot], tsend.at[0, slot], trecv.at[0, slot],
            peer("z", slot // 2, slot % 2)[1],
        )
        copy.start()
        sends.append(copy)
        totals_first.append(copy)
    index_copy.wait()
    for copy in weight_loads:
        copy.wait()

    def piece(g, slot, part, shift, core):
        return remote(
            q[g].at[slot, part], r1[g].at[slot, part], send1.at[g, slot], recv1.at[g, slot],
            peer(STAGES[g][0], shift, core)[1],
        )

    def step(s, carry):
        t = s // 2
        shift = lax.rem(t + 1, 4)
        core = 1 - lax.rem(s, 2)
        mine = shift * 2 + core

        def products(i, inner):
            for half in range(2):
                results = []
                for j in range(8):
                    block = jnp.clip(index_smem[0, mine * CHUNK + i * 16 + half * 8 + j], 0, BLOCKS)
                    results.append(
                        jnp.dot(
                            stack_ref[block],
                            weights_ref[jnp.minimum(block, BLOCKS - 1)],
                            preferred_element_type=F32,
                        )
                    )
                for j in range(8):
                    n = half * 8 + j
                    value = results[j]
                    st_a[pl.ds(i * 16 + n, 4, stride=64), :] = value[0:4]
                    st_b[pl.ds(i * 64 + n, 4, stride=16), :] = value[4:8]
                    st_c[pl.ds((n // 4) * 80 + i * 4 + n % 4, 5, stride=16), :] = value[8:13]
            return inner

        lax.fori_loop(0, 4, products, 0)
        whole = jnp.zeros((1, CELL), F32)
        for u in range(4):
            whole += encode(
                [st_a[r * 64 + u * 16 : r * 64 + u * 16 + 16, :] for r in range(4)],
                u * 16,
                lambda r, v: q_a.__setitem__((mine, u, r), v),
            )
        cs[0, mine, 1:2, :] = whole

        @pl.when(s < 7)
        def _():
            remote(
                q_a.at[mine], r1_a.at[mine], send1.at[0, mine], recv1.at[0, mine],
                peer("z", shift, core)[1],
            ).start()

        for g in (1, 2):
            rows = ROWS[g]
            for u in range(4):
                base = u * rows * 16
                slot = u * 2 + core
                cs[g, slot, 1:2, :] += encode(
                    [stage[g][base + r * 16 : base + r * 16 + 16, :] for r in range(rows)],
                    t * 16,
                    lambda r, v: q[g].__setitem__((slot, t, r), v),
                )
                if u == 0:

                    @pl.when(core == 1)
                    def _():
                        piece(g, slot, t, u, core).start()

                else:
                    piece(g, slot, t, u, core).start()
        return carry

    lax.fori_loop(0, 8, step, 0)

    first = [[None] * 8 for _ in range(3)]
    first_codes = [[None] * 8 for _ in range(3)]
    for slot in range(1, 8):
        for g in range(3):
            device = peer(STAGES[g][0], slot // 2, slot % 2)[1]
            copy = remote(
                cs.at[g, slot], c1.at[g, slot], csend.at[g, slot], crecv.at[g, slot], device
            )
            copy.start()
            first_codes[g][slot] = copy
            first[g][slot] = remote(
                q[g].at[slot], r1[g].at[slot], send1.at[g, slot], recv1.at[g, slot], device
            )
            sends += [copy, first[g][slot]]

    total = t_send[0]
    for slot, copy in enumerate(totals_first):
        copy.wait_recv()
        total += t1[slot + 1]
    t_send[1] = total
    totals_second = []
    for shift in (1, 2, 3):
        copy = remote(
            t_send.at[1], t2.at[shift - 1], tsend.at[1, shift], trecv.at[1, shift],
            peer("x", shift)[1],
        )
        copy.start()
        sends.append(copy)
        totals_second.append(copy)

    def join(rows):
        return jnp.concatenate(
            [jnp.where(low, rows[2 * p], rows[2 * p + 1]) for p in range(len(rows) // 2)], axis=1
        )

    second = []
    for g in range(3):
        for slot in range(1, 8):
            first_codes[g][slot].wait_recv()
            first[g][slot].wait_recv()
        heads = [cs[g, 0]] + [c1[g, slot] for slot in range(1, 8)]
        codes = join([h[0:1] for h in heads])
        scales = join([h[1:2] for h in heads])
        rows = lax.broadcasted_iota(jnp.int32, (256, 512), 0).astype(F32)
        select = jnp.where(rows == codes, scales, 0.0).astype(BF16)
        for row in range(ROWS[g]):
            data = jnp.concatenate(
                [
                    (q[g] if slot == 0 else r1[g])[slot, part, row]
                    for slot in range(8)
                    for part in range(4)
                ],
                axis=0,
            )
            both = jnp.dot(select, decode(data), preferred_element_type=F32)
            s2[g][row] = both[:, :CELL] + both[:, CELL:]
        for part in range(4):
            whole = jnp.zeros((1, CELL), F32)
            for u in range(4):
                base = part * 64 + u * 16
                whole += encode(
                    [s2[g][r, base : base + 16, :] for r in range(ROWS[g])],
                    u * 16,
                    lambda r, v: q2[g].__setitem__((part, u, r), v),
                )
            cs2[g, part, 0:1, :] = whole
        dim = STAGES[g][1]
        copies = []
        for shift in (2, 1, 3):
            at, device = peer(dim, shift)
            for src, dst, a, b in (
                (cs2.at[g, at[dim]], c2.at[g, shift], c2send, c2recv),
                (q2[g].at[at[dim]], r2[g].at[shift], send2, recv2),
            ):
                copy = remote(src, dst, a.at[g, shift], b.at[g, shift], device)
                copy.start()
                copies.append(copy)
        sends += copies
        second.append(copies)

    total = t_send[1]
    for shift in (1, 2, 3):
        totals_second[shift - 1].wait_recv()
        total += t2[shift - 1]
    t_send[2] = total
    totals_third = []
    for shift in (1, 2, 3):
        copy = remote(
            t_send.at[2], t3.at[shift - 1], tsend.at[2, shift], trecv.at[2, shift],
            peer("y", shift)[1],
        )
        copy.start()
        sends.append(copy)
        totals_third.append(copy)

    third = []
    for g in range(3):
        for copy in second[g]:
            copy.wait_recv()
        mine = here[STAGES[g][1]]
        scales = join([cs2[g, mine, 0:1, :]] + [c2[g, shift, 0:1, :] for shift in (1, 2, 3)])
        rows = lax.broadcasted_iota(jnp.int32, (64, 256), 0)
        lanes = lax.broadcasted_iota(jnp.int32, (64, 256), 1) % CHUNK
        select = jnp.where(rows == lanes, scales, 0.0).astype(BF16)
        for row in range(ROWS[g]):
            data = jnp.concatenate(
                [q2[g][mine, part, row] for part in range(4)]
                + [r2[g][shift, part, row] for shift in (1, 2, 3) for part in range(4)],
                axis=0,
            )
            both = jnp.dot(select, decode(data), preferred_element_type=F32)
            summed = both[:, :CELL] + both[:, CELL:]
            for part in range(4):
                s3[g][part, row] = summed[part * TARGETS : (part + 1) * TARGETS]
        dim = STAGES[g][2]
        copies = []
        for shift in (2, 1, 3):
            at, device = peer(dim, shift)
            copy = remote(
                s3[g].at[at[dim]], r3[g].at[shift - 1], send3.at[g, shift], recv3.at[g, shift], device
            )
            copy.start()
            copies.append(copy)
        sends += copies
        third.append(copies)

    total = t_send[2]
    for shift in (1, 2, 3):
        totals_third[shift - 1].wait_recv()
        total += t3[shift - 1]
    total = jnp.sum(total, axis=1, keepdims=True)
    mean = total[0:12] / jnp.maximum(total[12:13], 1.0)
    for g in range(3):
        for copy in third[g]:
            copy.wait_recv()
        mine = here[STAGES[g][2]]
        for row in range(ROWS[g]):
            summed = s3[g][mine, row] + r3[g][0, row] + r3[g][1, row] + r3[g][2, row]
            final_ref[pl.ds((FIRST[g] + row) * TARGETS, TARGETS), :] = summed
    for t in range(TARGETS):
        numer = final_ref[pl.ds(t, 12, stride=TARGETS), :]
        fraction = final_ref[pl.ds(12 * TARGETS + t, 1), :]
        filled = numer + jnp.maximum(0.25 - fraction, 0.0) * mean
        out_ref[:, t * CELL : (t + 1) * CELL] = filled / jnp.maximum(fraction, 0.25)
    for copy in sends:
        copy.wait_send()


def body(fields, land_mask, intersection, send_slot, target_block, live_blocks):
    smem = pl.BlockSpec(memory_space=pltpu.SMEM)
    hbm = pl.BlockSpec(memory_space=pl.ANY)
    dma = pltpu.SemaphoreType.DMA
    vmem = pltpu.VMEM
    i16 = jnp.int16
    i32 = jnp.int32
    return pl.pallas_call(
        kernel,
        in_specs=[smem] + [hbm] * 5,
        out_specs=pl.BlockSpec(memory_space=pltpu.VMEM),
        out_shape=jax.ShapeDtypeStruct((12, TARGETS * CELL), F32),
        scratch_shapes=[vmem((1, BLOCKS), i32), vmem((1, BLOCKS), i32)]
        + [vmem((12, BLOCKS * CELL), BF16), vmem((BLOCKS, CELL), i32)]
        + [vmem((BLOCKS, CELL, CELL), BF16), vmem((BLOCKS + 1, 16, CELL), BF16)]
        + [vmem((1, 512), i32), pltpu.SMEM((1, 512), i32)]
        + [vmem((n, CELL), F32) for n in (576, 336, 384)]
        + [vmem((8, 4, r, 16, CELL), i16) for r in ROWS] * 2
        + [vmem((3, 8, 8, CELL), F32)] * 2
        + [vmem((r, 256, CELL), F32) for r in ROWS]
        + [vmem((4, 4, r, 16, CELL), i16) for r in ROWS] * 2
        + [vmem((3, 4, 8, CELL), F32)] * 2
        + [vmem((4, r, TARGETS, CELL), F32) for r in ROWS]
        + [vmem((3, r, TARGETS, CELL), F32) for r in ROWS]
        + [vmem((13 * TARGETS, CELL), F32)]
        + [vmem((3, 16, CELL), F32), vmem((8, 16, CELL), F32)]
        + [vmem((3, 16, CELL), F32), vmem((3, 16, CELL), F32)]
        + [dma((5,)), dma((WEIGHT_COPIES,))]
        + [dma((3, 8))] * 4
        + [dma((3, 4))] * 6
        + [dma((3, 8))] * 2,
        compiler_params=pltpu.CompilerParams(
            collective_id=0, has_side_effects=True, vmem_limit_bytes=40 * 1024 * 1024
        ),
        name="remap",
    )(
        live_blocks,
        send_slot.reshape(1, BLOCKS),
        target_block.reshape(1, BLOCKS),
        fields,
        land_mask.reshape(BLOCKS, CELL),
        intersection,
    )


def solution(mesh):
    axes = ("band", "sub")
    return jax.shard_map(
        body,
        mesh=mesh,
        in_specs=(P(None, axes), P(axes), P(axes, None, None), P(axes), P(axes), P(axes)),
        out_specs=P(None, axes),
        check_vma=False,
    )
```

time: 61 us -> 50.8 us (0.83)
  Pallas kernels: 56.4 us -> 42.3 us
  local copies, waits for them, and re-layouts: 1.57 us -> 7.52 us
  other arithmetic: 2.01 us -> 0 us
    pallas_call x2 -> x1, Pallas kernels: 56.4 us -> 42.3 us  [body(): pl.pallas_call(kernel, in_specs=[smem] + [hbm] * 5, out_specs=pl.BlockSpe...]
    unnamed x1 -> x11, local copies, waits for them, and re-layouts: 1.57 us -> 7.52 us
    add x2 -> x0, other arithmetic: 1.41 us -> none  [body(): (((c * 4 + at[o[0]]) * 4 + at[o[1]]) * 4 + at[o[2]]) * 4 + k]
where the time goes in v2:
time: 50.8 us; the launch traced here: 50.5 us
  Pallas kernels  42.3 us (83%)
  local copies, waits for them, and re-layouts  7.52 us (15%)
  between operations  0.67 us (1%)
    pallas_call x1, Pallas kernels, body(): pl.pallas_call(kernel, in_specs=[smem] + [hbm] * 5, out_specs=pl.BlockSpe...  42.3 us
    unnamed x11, local copies, waits for them, and re-layouts  7.52 us

profile of v2, /device:TPU:0, one launch (start us, length us, event | category | flops | bytes accessed | tf_op | source)
XLA Modules:
  0.0 50.5 jit_solution(12002426123587220968)
XLA Ops:
  0.7 0.0 copy-start
  0.7 3.4 %copy-done = bf16[256,128,128]{2,1,0:T(8,128)(2,1)S(1)} copy-done((bf16[256,128,128]{2,1,0:T(8,128)(2,1)S(1)}, bf16[256,128,128]{2,1,0:T(8,128)(2,1)}, u32[]{:S(2)}) %copy-start) | copy-done | bytes 8388632
  4.0 0.0 copy-start.1
  4.0 1.2 %copy-done.1 = bf16[12,32768]{1,0:T(8,128)(2,1)S(1)} copy-done((bf16[12,32768]{1,0:T(8,128)(2,1)S(1)}, bf16[12,32768]{1,0:T(8,128)(2,1)}, u32[]{:S(2)}) %copy-start.1) | copy-done | bytes 786456
  5.3 0.0 copy-start.2
  5.3 0.9 %copy-done.2 = s32[32768]{0:T(1024)S(1)} copy-done((s32[32768]{0:T(1024)S(1)}, s32[32768]{0:T(1024)}, u32[]{:S(2)}) %copy-start.2) | copy-done | bytes 131096
  6.2 0.0 copy-start.3
  6.2 0.7 %copy-done.3 = s32[256]{0:T(256)S(1)} copy-done((s32[256]{0:T(256)S(1)}, s32[256]{0:T(256)}, u32[]{:S(2)}) %copy-start.3) | copy-done | bytes 1048
  6.8 0.0 copy-start.4
  6.8 0.7 %copy-done.4 = s32[256]{0:T(256)S(1)} copy-done((s32[256]{0:T(256)S(1)}, s32[256]{0:T(256)}, u32[]{:S(2)}) %copy-start.4) | copy-done | bytes 1048
  7.5 42.3 %remap.1 = f32[12,2048]{1,0:T(8,128)S(1)} custom-call(s32[1]{0:T(128)S(6)} %copy.8.live_ref, s32[1,256]{1,0:T(1,128)S(1)} %bitcast.4, s32[1,256]{1,0:T(1,128)S(1)} %bitcast.5, bf16[12,32768]{1,0:T(8,128)(2,1)S(1)} %copy-done.1, s32[256,128]{1,0:T(8,128)S(1)} %bitcast.3, bf16[256,128,128]{2,1,0:T(8,128)(2,1)S(1)} %copy-done), custom_call_target="tpu_custom_call" | custom-call | tf_op jit(solution)/shard_map/remap/pallas_call | solution.py:413
  49.9 0.7 %copy.9 = f32[12,2048]{1,0:T(8,128)} copy(f32[12,2048]{1,0:T(8,128)S(1)} %remap.1) | data formatting | bytes 196608
Async XLA Ops:
  0.7 3.4 %copy-start = (bf16[256,128,128]{2,1,0:T(8,128)(2,1)S(1)}, bf16[256,128,128]{2,1,0:T(8,128)(2,1)}, u32[]{:S(2)}) copy-start(bf16[256,128,128]{2,1,0:T(8,128)(2,1)} %weights_hbm.1) | copy-start | bytes 25165828
  4.0 1.2 %copy-start.1 = (bf16[12,32768]{1,0:T(8,128)(2,1)S(1)}, bf16[12,32768]{1,0:T(8,128)(2,1)}, u32[]{:S(2)}) copy-start(bf16[12,32768]{1,0:T(8,128)(2,1)} %fields_hbm.1) | copy-start | bytes 2359300
  5.3 0.9 %copy-start.2 = (s32[32768]{0:T(1024)S(1)}, s32[32768]{0:T(1024)}, u32[]{:S(2)}) copy-start(s32[32768]{0:T(1024)} %param.7) | copy-start | bytes 393220
  6.2 0.7 %copy-start.3 = (s32[256]{0:T(256)S(1)}, s32[256]{0:T(256)}, u32[]{:S(2)}) copy-start(s32[256]{0:T(256)} %param.9) | copy-start | bytes 3076
  6.8 0.7 %copy-start.4 = (s32[256]{0:T(256)S(1)}, s32[256]{0:T(256)}, u32[]{:S(2)}) copy-start(s32[256]{0:T(256)} %param.10) | copy-start | bytes 3076

commit v3 on v2

v3 whole, which is shorter than its diff:
```python
import jax
import jax.numpy as jnp
from jax import lax
from jax.experimental import pallas as pl
from jax.experimental.pallas import tpu as pltpu
from jax.sharding import PartitionSpec as P

CELL = 128
BLOCKS = 256
TARGETS = 16
CHUNK = 64
ROWS = (4, 4, 5)
FIRST = (0, 4, 8)
STAGES = ("zxy", "xyz", "yzx")
SLOTS = ("zxy", "xzy", "yzx")
MESH = pl.DeviceIdType.MESH
F32 = jnp.float32
BF16 = jnp.bfloat16
WEIGHT_COPIES = 4


def encode(tiles, write):
    top = jnp.abs(tiles[0])
    for tile in tiles[1:]:
        top = jnp.maximum(top, jnp.abs(tile))
    top = jnp.maximum(jnp.max(top, axis=1, keepdims=True), 1e-25)
    power = jnp.ceil(jnp.log2(top) + 0.02)
    down = jnp.exp2(-power)
    for row, tile in enumerate(tiles):
        small = tile * down
        code = small * lax.rsqrt(jnp.abs(small) + 1e-30) * 32768.0
        write(row, jnp.round(code).astype(jnp.int32).astype(jnp.int16))
    return jnp.exp2(power - 30.0)


def spread(scale, period, lane):
    lanes = lax.broadcasted_iota(jnp.int32, (16, CELL), 1) % period
    slots = lax.broadcasted_iota(jnp.int32, (16, CELL), 0) + lane
    return jnp.sum(jnp.where(lanes == slots, scale, 0.0), axis=0, keepdims=True)


def decode(codes):
    value = codes.astype(F32)
    value = value * jnp.abs(value)
    high = value.astype(BF16)
    return jnp.concatenate([high, (value - high.astype(F32)).astype(BF16)], axis=1)


def kernel(
    live_ref, slot_hbm, target_hbm, fields_hbm, mask_hbm, weights_hbm, out_ref,
    slot_ref, target_ref, fields_ref, mask_ref, weights_ref, stack_ref, index_vmem, index_smem,
    even_a, even_b, even_c, odd_a, odd_b, odd_c, q_a, q_b, q_c, r1_a, r1_b, r1_c, cs, c1,
    s2_a, s2_b, s2_c, q2_a, q2_b, q2_c, r2_a, r2_b, r2_c, cs2, c2, final_ref, t_send, t1, t2,
    load, wload, send1, recv1, csend, crecv, send2, recv2, c2send, c2recv, tsend, trecv,
):
    stages = ((even_a, even_b, even_c), (odd_a, odd_b, odd_c))
    q = (q_a, q_b, q_c)
    r1 = (r1_a, r1_b, r1_c)
    s2 = (s2_a, s2_b, s2_c)
    q2 = (q2_a, q2_b, q2_c)
    r2 = (r2_a, r2_b, r2_c)
    band = lax.axis_index("band")
    here = {
        "y": band // 8,
        "x": lax.rem(band // 2, 4),
        "c": lax.rem(band, 2),
        "z": lax.axis_index("sub"),
    }

    def peer(**shifts):
        at = {}
        for dim in "yxcz":
            at[dim] = here[dim]
            if dim in shifts:
                at[dim] = lax.rem(here[dim] + shifts[dim], 2 if dim == "c" else 4)
        return at, ((at["y"] * 4 + at["x"]) * 2 + at["c"], at["z"])

    def remote(src, dst, send, recv, device):
        return pltpu.make_async_remote_copy(
            src_ref=src, dst_ref=dst, send_sem=send, recv_sem=recv,
            device_id=device, device_id_type=MESH,
        )

    partner = peer(c=1)[1]

    loads = [
        pltpu.make_async_copy(slot_hbm, slot_ref, load.at[0]),
        pltpu.make_async_copy(target_hbm, target_ref, load.at[1]),
        pltpu.make_async_copy(mask_hbm, mask_ref, load.at[2]),
        pltpu.make_async_copy(fields_hbm, fields_ref, load.at[3]),
    ]
    size = BLOCKS // WEIGHT_COPIES
    weight_loads = [
        pltpu.make_async_copy(
            weights_hbm.at[pl.ds(i * size, size)], weights_ref.at[pl.ds(i * size, size)], wload.at[i]
        )
        for i in range(WEIGHT_COPIES)
    ]
    for copy in loads + weight_loads:
        copy.start()

    barrier = pltpu.get_barrier_semaphore()
    greeted = set()
    for g in range(3):
        first, second, third = STAGES[g]
        for n in range(1, 8):
            greeted.add(tuple(sorted({first: n // 2, "c": n % 2}.items())))
        for n in range(1, 16):
            greeted.add(tuple(sorted({second: n // 4, third: n % 4}.items())))
    greeted = {tuple(item for item in names if item[1]) for names in greeted}
    for names in sorted(greeted):
        pl.semaphore_signal(
            barrier, inc=1, device_id=peer(**dict(names))[1], device_id_type=MESH
        )

    low = lax.broadcasted_iota(jnp.int32, (1, CELL), 1) < CHUNK
    blocks = lax.broadcasted_iota(jnp.int32, (8, BLOCKS), 1)
    kind = lax.broadcasted_iota(jnp.int32, (8, BLOCKS), 0)
    place = lax.broadcasted_iota(jnp.int32, (512, 1), 0)
    along = lax.broadcasted_iota(jnp.int32, (1, 512), 1)
    cs[...] = jnp.zeros_like(cs)
    loads[0].wait()
    loads[1].wait()
    facts = jnp.where(kind == 0, blocks - BLOCKS, jnp.broadcast_to(target_ref[...], (8, BLOCKS)))
    facts = facts.astype(F32).astype(BF16)
    for g in range(3):
        order = SLOTS[g]

        def split(n):
            chunk, second, third, k = n // 64, (n // 16) % 4, (n // 4) % 4, n % 4
            if g > 0:
                second = second + 1
            at = {
                order[0]: (here[order[0]] + chunk // 2) % 4,
                order[1]: (here[order[1]] + second) % 4,
                order[2]: (here[order[2]] + third) % 4,
                "c": (here["c"] + chunk) % 2,
            }
            return at, k

        at, k = split(place)
        wanted = (((at["y"] * 4 + at["x"]) * 2 + at["c"]) * 4 + at["z"]) * 4 + k
        hits = jnp.where(wanted == slot_ref[...], 1.0, 0.0).astype(BF16)
        found = lax.dot_general(
            facts, hits, (((1,), (1,)), ((), ())), preferred_element_type=F32
        )
        if g == 0:
            index_vmem[...] = (found[0:1] + BLOCKS).astype(jnp.int32)
            index_copy = pltpu.make_async_copy(index_vmem, index_smem, load.at[4])
            index_copy.start()
        at, k = split(along)
        owner = at[STAGES[g][1]] * 4 + at[STAGES[g][2]]
        code = found[1:2] + (owner * TARGETS).astype(F32)
        for pair in range(4):
            both = code[:, pair * CELL : (pair + 1) * CELL]
            rolled = pltpu.roll(both, CHUNK, 1)
            cs[g, 2 * pair, 0:1, :] = jnp.where(low, both, rolled)
            cs[g, 2 * pair + 1, 0:1, :] = jnp.where(low, rolled, both)

    loads[2].wait()
    loads[3].wait()
    live = live_ref[0]

    def build(i, total):
        for j in range(8):
            block = i * 8 + j
            alive = (block < live).astype(jnp.int32)
            mask = (mask_ref[pl.ds(block, 1), :] * alive).astype(F32)
            values = fields_ref[:, pl.ds(pl.multiple_of(block * CELL, CELL), CELL)].astype(F32)
            stacked = jnp.concatenate([values * mask, jnp.broadcast_to(mask, (4, CELL))], axis=0)
            total += stacked
            stack_ref[block] = stacked.astype(BF16)
        return total

    total = lax.fori_loop(0, BLOCKS // 8, build, jnp.zeros((16, CELL), F32))
    stack_ref[BLOCKS] = jnp.zeros((16, CELL), BF16)
    t_send[0] = total
    pl.semaphore_wait(barrier, len(greeted))

    for slot in range(1, 8):
        remote(
            t_send.at[0], t1.at[slot], tsend.at[0], trecv.at[0], peer(z=slot // 2, c=slot % 2)[1]
        ).start()
    index_copy.wait()
    for copy in weight_loads:
        copy.wait()

    def products(t, core, group):
        mine = lax.rem(t + 1, 4) * 2 + core
        stage = stages[core]
        results = []
        for j in range(8):
            at = mine * CHUNK + group * 8 + j
            block = jnp.clip(index_smem[0, at], 0, BLOCKS)
            results.append(
                jnp.dot(
                    stack_ref[block],
                    weights_ref[jnp.minimum(block, BLOCKS - 1)],
                    preferred_element_type=F32,
                )
            )
        for j in range(8):
            i, n = group // 2, (group % 2) * 8 + j
            value = results[j]
            stage[0][pl.ds(i * 16 + n, 4, stride=64), :] = value[0:4]
            stage[1][pl.ds(i * 64 + n, 4, stride=16), :] = value[4:8]
            stage[2][pl.ds((n // 4) * 80 + i * 4 + n % 4, 5, stride=16), :] = value[8:13]

    def code_tile(t, core, g, u, rows):
        stage = stages[core][g]
        if g == 0:
            mine = lax.rem(t + 1, 4) * 2 + core
            scale = encode(
                [stage[r * 64 + u * 16 : r * 64 + u * 16 + 16, :] for r in range(4)],
                lambda r, v: q_a.__setitem__((mine, u, r), v),
            )
            rows.append(spread(scale, CHUNK, u * 16))
        else:
            base = u * ROWS[g] * 16
            slot = u * 2 + core
            scale = encode(
                [stage[base + r * 16 : base + r * 16 + 16, :] for r in range(ROWS[g])],
                lambda r, v: q[g].__setitem__((slot, t, r), v),
            )
            cs[g, slot, 1:2, :] += spread(scale, CHUNK, t * 16)

    def ship(t, core, rows, home):
        shift = lax.rem(t + 1, 4)
        mine = shift * 2 + core
        cs[0, mine, 1:2, :] = (rows[0] + rows[1]) + (rows[2] + rows[3])
        if not home:
            remote(
                q_a.at[mine], r1_a.at[mine], send1.at[0], recv1.at[0], peer(z=shift, c=core)[1]
            ).start()
        for u in (2, 1, 3, 0):
            for g in (1, 2):
                if u or core:
                    slot = u * 2 + core
                    remote(
                        q[g].at[slot, t], r1[g].at[slot, t], send1.at[g], recv1.at[g],
                        peer(**{STAGES[g][0]: u, "c": core})[1],
                    ).start()

    tiles = [(g, u) for g in range(3) for u in range(4)]

    def together(ahead, behind, home=False):
        rows = []
        done = 0
        for group in range(8):
            if ahead is not None:
                products(*ahead, group)
            if behind is not None:
                upto = (group + 1) * len(tiles) // 8
                for g, u in tiles[done:upto]:
                    code_tile(*behind, g, u, rows)
                done = upto
        if behind is not None:
            ship(*behind, rows, home)

    together((0, 1), None)

    def step(t, carry):
        together((t, 0), (t, 1))
        together((t + 1, 1), (t, 0))
        return carry

    lax.fori_loop(0, 3, step, 0)
    together((3, 0), (3, 1))
    together(None, (3, 0), home=True)

    for slot in range(1, 8):
        for g in range(3):
            remote(
                cs.at[g, slot], c1.at[g, slot], csend.at[g], crecv.at[g],
                peer(**{STAGES[g][0]: slot // 2, "c": slot % 2})[1],
            ).start()

    def batch(src, dst, send, recv):
        return remote(src, dst, send, recv, partner)

    rest = pl.ds(1, 7)
    sums_first = batch(t1.at[rest], t1.at[rest], tsend.at[0], trecv.at[0])
    sums_first.wait_recv()
    total = t_send[0]
    for slot in range(1, 8):
        total += t1[slot]
    t_send[1] = total
    far = sorted(range(1, 16), key=lambda n: -(min(n // 4, 4 - n // 4) + min(n % 4, 4 - n % 4)))
    for n in far:
        remote(
            t_send.at[1], t2.at[n], tsend.at[1], trecv.at[1], peer(x=n // 4, y=n % 4)[1]
        ).start()

    ends = [sums_first]
    others = pl.ds(1, 15)
    for g in range(3):
        heads = batch(cs.at[g, rest], c1.at[g, rest], csend.at[g], crecv.at[g])
        datas = batch(q[g].at[rest], r1[g].at[rest], send1.at[g], recv1.at[g])
        heads.wait_recv()
        datas.wait_recv()
        ends += [heads, datas]
        head = [cs[g, 0]] + [c1[g, slot] for slot in range(1, 8)]

        def lane_row(at):
            return jnp.concatenate(
                [
                    jnp.where(low, head[2 * p][at : at + 1], head[2 * p + 1][at : at + 1])
                    for p in range(4)
                ],
                axis=1,
            )

        rows = lax.broadcasted_iota(jnp.int32, (256, 512), 0).astype(F32)
        select = jnp.where(rows == lane_row(0), lane_row(1), 0.0).astype(BF16)
        for row in range(ROWS[g]):
            data = jnp.concatenate(
                [
                    (q[g] if slot == 0 else r1[g])[slot, part, row]
                    for slot in range(8)
                    for part in range(4)
                ],
                axis=0,
            )
            both = jnp.dot(select, decode(data), preferred_element_type=F32)
            s2[g][row] = both[:, :CELL] + both[:, CELL:]
        for owner in range(16):
            scale = encode(
                [s2[g][r, owner * 16 : owner * 16 + 16, :] for r in range(ROWS[g])],
                lambda r, v: q2[g].__setitem__((owner, r), v),
            )
            cs2[g, owner, 0:1, :] = spread(scale, 16, 0)
        second, third = STAGES[g][1:]
        for n in far:
            at, device = peer(**{second: n // 4, third: n % 4})
            owner = at[second] * 4 + at[third]
            remote(
                cs2.at[g, owner], c2.at[g, n], c2send.at[g], c2recv.at[g], device
            ).start()
            remote(q2[g].at[owner], r2[g].at[n], send2.at[g], recv2.at[g], device).start()

    sums_second = batch(t2.at[others], t2.at[others], tsend.at[1], trecv.at[1])
    sums_second.wait_recv()
    ends.append(sums_second)
    total = t_send[1]
    for n in range(1, 16):
        total += t2[n]
    total = jnp.sum(total, axis=1, keepdims=True)
    mean = total[0:12] / jnp.maximum(total[12:13], 1.0)
    group_of = lax.broadcasted_iota(jnp.int32, (1, CELL), 1) // 16
    for g in range(3):
        heads = batch(c2.at[g, others], c2.at[g, others], c2send.at[g], c2recv.at[g])
        datas = batch(r2[g].at[others], r2[g].at[others], send2.at[g], recv2.at[g])
        heads.wait_recv()
        datas.wait_recv()
        ends += [heads, datas]
        mine = here[STAGES[g][1]] * 4 + here[STAGES[g][2]]
        halves = []
        for half in range(2):
            row = jnp.zeros((1, CELL), F32)
            for n in range(8):
                source = cs2[g, mine, 0:1, :] if half + n == 0 else c2[g, half * 8 + n, 0:1, :]
                row = jnp.where(group_of == n, source, row)
            halves.append(row)
        scales = jnp.concatenate(halves, axis=1)
        rows = lax.broadcasted_iota(jnp.int32, (16, 256), 0)
        lanes = lax.broadcasted_iota(jnp.int32, (16, 256), 1) % 16
        select = jnp.where(rows == lanes, scales, 0.0).astype(BF16)
        for row in range(ROWS[g]):
            data = jnp.concatenate(
                [q2[g][mine, row]] + [r2[g][n, row] for n in range(1, 16)], axis=0
            )
            both = jnp.dot(select, decode(data), preferred_element_type=F32)
            final_ref[pl.ds((FIRST[g] + row) * TARGETS, TARGETS), :] = (
                both[:, :CELL] + both[:, CELL:]
            )
    for t in range(TARGETS):
        numer = final_ref[pl.ds(t, 12, stride=TARGETS), :]
        fraction = final_ref[pl.ds(12 * TARGETS + t, 1), :]
        filled = numer + jnp.maximum(0.25 - fraction, 0.0) * mean
        out_ref[:, t * CELL : (t + 1) * CELL] = filled / jnp.maximum(fraction, 0.25)
    for copy in ends:
        copy.wait_send()


def body(fields, land_mask, intersection, send_slot, target_block, live_blocks):
    smem = pl.BlockSpec(memory_space=pltpu.SMEM)
    hbm = pl.BlockSpec(memory_space=pl.ANY)
    dma = pltpu.SemaphoreType.DMA
    vmem = pltpu.VMEM
    i16 = jnp.int16
    i32 = jnp.int32
    return pl.pallas_call(
        kernel,
        in_specs=[smem] + [hbm] * 5,
        out_specs=pl.BlockSpec(memory_space=pltpu.VMEM),
        out_shape=jax.ShapeDtypeStruct((12, TARGETS * CELL), F32),
        scratch_shapes=[vmem((1, BLOCKS), i32), vmem((1, BLOCKS), i32)]
        + [vmem((12, BLOCKS * CELL), BF16), vmem((BLOCKS, CELL), i32)]
        + [vmem((BLOCKS, CELL, CELL), BF16), vmem((BLOCKS + 1, 16, CELL), BF16)]
        + [vmem((1, 512), i32), pltpu.SMEM((1, 512), i32)]
        + [vmem((n, CELL), F32) for n in (576, 336, 384)] * 2
        + [vmem((8, 4, r, 16, CELL), i16) for r in ROWS] * 2
        + [vmem((3, 8, 8, CELL), F32)] * 2
        + [vmem((r, 256, CELL), F32) for r in ROWS]
        + [vmem((16, r, 16, CELL), i16) for r in ROWS] * 2
        + [vmem((3, 16, 8, CELL), F32)] * 2
        + [vmem((16 * TARGETS, CELL), F32)]
        + [vmem((2, 16, CELL), F32), vmem((8, 16, CELL), F32), vmem((16, 16, CELL), F32)]
        + [dma((5,)), dma((WEIGHT_COPIES,))]
        + [dma((3,))] * 8
        + [dma((2,))] * 2,
        compiler_params=pltpu.CompilerParams(
            collective_id=0, has_side_effects=True, vmem_limit_bytes=62 * 1024 * 1024
        ),
        name="remap",
    )(
        live_blocks,
        send_slot.reshape(1, BLOCKS),
        target_block.reshape(1, BLOCKS),
        fields,
        land_mask.reshape(BLOCKS, CELL),
        intersection,
    )


def solution(mesh):
    axes = ("band", "sub")
    return jax.shard_map(
        body,
        mesh=mesh,
        in_specs=(P(None, axes), P(axes), P(axes, None, None), P(axes), P(axes), P(axes)),
        out_specs=P(None, axes),
        check_vma=False,
    )
```

time: 50.8 us -> 36 us (0.71)
  Pallas kernels: 42.3 us -> 33.2 us
  local copies, waits for them, and re-layouts: 7.52 us -> 1.57 us
    pallas_call x1, Pallas kernels: 42.3 us -> 33.2 us  [body(): pl.pallas_call(kernel, in_specs=[smem] + [hbm] * 5, out_specs=pl.BlockSpe...]
    unnamed x11 -> x1, local copies, waits for them, and re-layouts: 7.52 us -> 1.57 us
where the time goes in v3:
time: 36 us; the launch traced here: 35.4 us
  Pallas kernels  33.2 us (92%)
  local copies, waits for them, and re-layouts  1.57 us (4%)
  between operations  0.66 us (2%)
    pallas_call x1, Pallas kernels, body(): pl.pallas_call(kernel, in_specs=[smem] + [hbm] * 5, out_specs=pl.BlockSpe...  33.2 us
    unnamed x1, local copies, waits for them, and re-layouts  1.57 us

profile of v3, /device:TPU:0, one launch (start us, length us, event | category | flops | bytes accessed | tf_op | source)
XLA Modules:
  0.0 35.4 jit_solution(729837567336945814)
XLA Ops:
  0.7 33.2 %remap.1 = f32[12,2048]{1,0:T(8,128)} custom-call(s32[1]{0:T(128)S(6)} %copy.8.live_ref, s32[1,256]{1,0:T(1,128)} %bitcast.4, s32[1,256]{1,0:T(1,128)} %bitcast.5, bf16[12,32768]{1,0:T(8,128)(2,1)} %fields_hbm.1, s32[256,128]{1,0:T(8,128)} %bitcast.3, bf16[256,128,128]{2,1,0:T(8,128)(2,1)} %weights_hbm.1), custom_call_target="tpu_custom_call" | custom-call | tf_op jit(solution)/shard_map/remap/pallas_call | solution.py:392
  33.8 1.6 %copy.9 = f32[12,2048]{1,0:T(8,128)} copy(f32[12,2048]{1,0:T(8,128)} %remap.1) | data formatting | bytes 196608

commit v4 on v3

--- a/solution.py
+++ b/solution.py
@@ -83,6 +83,10 @@
 
     partner = peer(c=1)[1]
 
+    def reach(t):
+        near = 1 + 2 * here["c"]
+        return jnp.where(t == 0, 2, jnp.where(t == 1, near, jnp.where(t == 2, 4 - near, 0)))
+
     loads = [
         pltpu.make_async_copy(slot_hbm, slot_ref, load.at[0]),
         pltpu.make_async_copy(target_hbm, target_ref, load.at[1]),
@@ -123,13 +127,15 @@
     loads[1].wait()
     facts = jnp.where(kind == 0, blocks - BLOCKS, jnp.broadcast_to(target_ref[...], (8, BLOCKS)))
     facts = facts.astype(F32).astype(BF16)
-    for g in range(3):
+    index_copy = pltpu.make_async_copy(index_vmem, index_smem, load.at[4])
+
+    def fill(g):
         order = SLOTS[g]
 
         def split(n):
             chunk, second, third, k = n // 64, (n // 16) % 4, (n // 4) % 4, n % 4
             if g > 0:
-                second = second + 1
+                second = reach(second)
             at = {
                 order[0]: (here[order[0]] + chunk // 2) % 4,
                 order[1]: (here[order[1]] + second) % 4,
@@ -146,7 +152,6 @@
         )
         if g == 0:
             index_vmem[...] = (found[0:1] + BLOCKS).astype(jnp.int32)
-            index_copy = pltpu.make_async_copy(index_vmem, index_smem, load.at[4])
             index_copy.start()
         at, k = split(along)
         owner = at[STAGES[g][1]] * 4 + at[STAGES[g][2]]
@@ -156,6 +161,8 @@
             rolled = pltpu.roll(both, CHUNK, 1)
             cs[g, 2 * pair, 0:1, :] = jnp.where(low, both, rolled)
             cs[g, 2 * pair + 1, 0:1, :] = jnp.where(low, rolled, both)
+
+    fill(0)
 
     loads[2].wait()
     loads[3].wait()
@@ -174,7 +181,7 @@
 
     total = lax.fori_loop(0, BLOCKS // 8, build, jnp.zeros((16, CELL), F32))
     stack_ref[BLOCKS] = jnp.zeros((16, CELL), BF16)
-    t_send[0] = total
+    t_send[0] = spread(jnp.sum(total, axis=1, keepdims=True), CELL, 0)
     pl.semaphore_wait(barrier, len(greeted))
 
     for slot in range(1, 8):
@@ -186,7 +193,7 @@
         copy.wait()
 
     def products(t, core, group):
-        mine = lax.rem(t + 1, 4) * 2 + core
+        mine = reach(t) * 2 + core
         stage = stages[core]
         results = []
         for j in range(8):
@@ -209,7 +216,7 @@
     def code_tile(t, core, g, u, rows):
         stage = stages[core][g]
         if g == 0:
-            mine = lax.rem(t + 1, 4) * 2 + core
+            mine = reach(t) * 2 + core
             scale = encode(
                 [stage[r * 64 + u * 16 : r * 64 + u * 16 + 16, :] for r in range(4)],
                 lambda r, v: q_a.__setitem__((mine, u, r), v),
@@ -225,10 +232,13 @@
             cs[g, slot, 1:2, :] += spread(scale, CHUNK, t * 16)
 
     def ship(t, core, rows, home):
-        shift = lax.rem(t + 1, 4)
+        shift = reach(t)
         mine = shift * 2 + core
         cs[0, mine, 1:2, :] = (rows[0] + rows[1]) + (rows[2] + rows[3])
         if not home:
+            remote(
+                cs.at[0, mine], c1.at[0, mine], csend.at[0], crecv.at[0], peer(z=shift, c=core)[1]
+            ).start()
             remote(
                 q_a.at[mine], r1_a.at[mine], send1.at[0], recv1.at[0], peer(z=shift, c=core)[1]
             ).start()
@@ -243,12 +253,14 @@
 
     tiles = [(g, u) for g in range(3) for u in range(4)]
 
-    def together(ahead, behind, home=False):
+    def together(ahead, behind, home=False, extra=False):
         rows = []
         done = 0
         for group in range(8):
             if ahead is not None:
                 products(*ahead, group)
+            if extra and group in (2, 5):
+                fill(1 + group // 5)
             if behind is not None:
                 upto = (group + 1) * len(tiles) // 8
                 for g, u in tiles[done:upto]:
@@ -257,7 +269,7 @@
         if behind is not None:
             ship(*behind, rows, home)
 
-    together((0, 1), None)
+    together((0, 1), None, extra=True)
 
     def step(t, carry):
         together((t, 0), (t, 1))
@@ -269,7 +281,7 @@
     together(None, (3, 0), home=True)
 
     for slot in range(1, 8):
-        for g in range(3):
+        for g in (1, 2):
             remote(
                 cs.at[g, slot], c1.at[g, slot], csend.at[g], crecv.at[g],
                 peer(**{STAGES[g][0]: slot // 2, "c": slot % 2})[1],
@@ -344,7 +356,9 @@
     total = t_send[1]
     for n in range(1, 16):
         total += t2[n]
-    total = jnp.sum(total, axis=1, keepdims=True)
+    lanes = lax.broadcasted_iota(jnp.int32, (16, CELL), 1)
+    rows = lax.broadcasted_iota(jnp.int32, (16, CELL), 0)
+    total = jnp.sum(jnp.where(lanes == rows, total, 0.0), axis=1, keepdims=True)
     mean = total[0:12] / jnp.maximum(total[12:13], 1.0)
     group_of = lax.broadcasted_iota(jnp.int32, (1, CELL), 1) // 16
     for g in range(3):
@@ -400,12 +414,12 @@
         + [vmem((1, 512), i32), pltpu.SMEM((1, 512), i32)]
         + [vmem((n, CELL), F32) for n in (576, 336, 384)] * 2
         + [vmem((8, 4, r, 16, CELL), i16) for r in ROWS] * 2
-        + [vmem((3, 8, 8, CELL), F32)] * 2
+        + [vmem((3, 8, 2, CELL), F32)] * 2
         + [vmem((r, 256, CELL), F32) for r in ROWS]
         + [vmem((16, r, 16, CELL), i16) for r in ROWS] * 2
-        + [vmem((3, 16, 8, CELL), F32)] * 2
+        + [vmem((3, 16, 1, CELL), F32)] * 2
         + [vmem((16 * TARGETS, CELL), F32)]
-        + [vmem((2, 16, CELL), F32), vmem((8, 16, CELL), F32), vmem((16, 16, CELL), F32)]
+        + [vmem((2, 1, CELL), F32), vmem((8, 1, CELL), F32), vmem((16, 1, CELL), F32)]
         + [dma((5,)), dma((WEIGHT_COPIES,))]
         + [dma((3,))] * 8
         + [dma((2,))] * 2,

time: 36 us -> 34 us (0.944)
  Pallas kernels: 33.2 us -> 31.4 us
    pallas_call x1, Pallas kernels: 33.2 us -> 31.4 us  [body(): pl.pallas_call(kernel, in_specs=[smem] + [hbm] * 5, out_specs=pl.BlockSpe...]
where the time goes in v4:
time: 34 us; the launch traced here: 33.6 us
  Pallas kernels  31.4 us (92%)
  local copies, waits for them, and re-layouts  1.57 us (5%)
  between operations  0.66 us (2%)
    pallas_call x1, Pallas kernels, body(): pl.pallas_call(kernel, in_specs=[smem] + [hbm] * 5, out_specs=pl.BlockSpe...  31.4 us
    unnamed x1, local copies, waits for them, and re-layouts  1.57 us

profile of v4, /device:TPU:0, one launch (start us, length us, event | category | flops | bytes accessed | tf_op | source)
XLA Modules:
  0.0 33.6 jit_solution(1804899248576651698)
XLA Ops:
  0.7 31.4 %remap.1 = f32[12,2048]{1,0:T(8,128)} custom-call(s32[1]{0:T(128)S(6)} %copy.8.live_ref, s32[1,256]{1,0:T(1,128)} %bitcast.4, s32[1,256]{1,0:T(1,128)} %bitcast.5, bf16[12,32768]{1,0:T(8,128)(2,1)} %fields_hbm.1, s32[256,128]{1,0:T(8,128)} %bitcast.3, bf16[256,128,128]{2,1,0:T(8,128)(2,1)} %weights_hbm.1), custom_call_target="tpu_custom_call" | custom-call | tf_op jit(solution)/shard_map/remap/pallas_call | solution.py:406
  32.1 1.6 %copy.9 = f32[12,2048]{1,0:T(8,128)} copy(f32[12,2048]{1,0:T(8,128)} %remap.1) | data formatting | bytes 196608

commit v5 on v4

--- a/solution.py
+++ b/solution.py
@@ -16,7 +16,7 @@
 MESH = pl.DeviceIdType.MESH
 F32 = jnp.float32
 BF16 = jnp.bfloat16
-WEIGHT_COPIES = 4
+WEIGHT_COPIES = 1
 
 
 def encode(tiles, write):
@@ -134,13 +134,16 @@
 
         def split(n):
             chunk, second, third, k = n // 64, (n // 16) % 4, (n // 4) % 4, n % 4
-            if g > 0:
-                second = reach(second)
+            if g == 0:
+                first, core = reach(chunk // 2), 1 - chunk % 2
+            else:
+                first, core = chunk // 2, chunk % 2
+                second = reach((second // 2 + core) % 2 * 2 + second % 2)
             at = {
-                order[0]: (here[order[0]] + chunk // 2) % 4,
+                order[0]: (here[order[0]] + first) % 4,
                 order[1]: (here[order[1]] + second) % 4,
                 order[2]: (here[order[2]] + third) % 4,
-                "c": (here["c"] + chunk) % 2,
+                "c": (here["c"] + core) % 2,
             }
             return at, k
 
@@ -159,8 +162,9 @@
         for pair in range(4):
             both = code[:, pair * CELL : (pair + 1) * CELL]
             rolled = pltpu.roll(both, CHUNK, 1)
-            cs[g, 2 * pair, 0:1, :] = jnp.where(low, both, rolled)
-            cs[g, 2 * pair + 1, 0:1, :] = jnp.where(low, rolled, both)
+            for half in range(2 if g else 1):
+                cs[half, g, 2 * pair, 0:1, :] = jnp.where(low, both, rolled)
+                cs[half, g, 2 * pair + 1, 0:1, :] = jnp.where(low, rolled, both)
 
     fill(0)
 
@@ -182,6 +186,8 @@
     total = lax.fori_loop(0, BLOCKS // 8, build, jnp.zeros((16, CELL), F32))
     stack_ref[BLOCKS] = jnp.zeros((16, CELL), BF16)
     t_send[0] = spread(jnp.sum(total, axis=1, keepdims=True), CELL, 0)
+    fill(1)
+    fill(2)
     pl.semaphore_wait(barrier, len(greeted))
 
     for slot in range(1, 8):
@@ -193,7 +199,7 @@
         copy.wait()
 
     def products(t, core, group):
-        mine = reach(t) * 2 + core
+        mine = t * 2 + 1 - core
         stage = stages[core]
         results = []
         for j in range(8):
@@ -216,7 +222,7 @@
     def code_tile(t, core, g, u, rows):
         stage = stages[core][g]
         if g == 0:
-            mine = reach(t) * 2 + core
+            mine = t * 2 + 1 - core
             scale = encode(
                 [stage[r * 64 + u * 16 : r * 64 + u * 16 + 16, :] for r in range(4)],
                 lambda r, v: q_a.__setitem__((mine, u, r), v),
@@ -229,38 +235,46 @@
                 [stage[base + r * 16 : base + r * 16 + 16, :] for r in range(ROWS[g])],
                 lambda r, v: q[g].__setitem__((slot, t, r), v),
             )
-            cs[g, slot, 1:2, :] += spread(scale, CHUNK, t * 16)
+            half = t // 2
+            lane = lax.rem(half + core, 2) * 32 + lax.rem(t, 2) * 16
+            cs[half, g, slot, 1:2, :] += spread(scale, CHUNK, lane)
 
     def ship(t, core, rows, home):
-        shift = reach(t)
-        mine = shift * 2 + core
-        cs[0, mine, 1:2, :] = (rows[0] + rows[1]) + (rows[2] + rows[3])
+        half = t // 2
+        mine = t * 2 + 1 - core
+        cs[0, 0, mine, 1:2, :] = (rows[0] + rows[1]) + (rows[2] + rows[3])
         if not home:
+            device = peer(z=reach(t), c=core)[1]
             remote(
-                cs.at[0, mine], c1.at[0, mine], csend.at[0], crecv.at[0], peer(z=shift, c=core)[1]
+                cs.at[0, 0, mine], c1.at[0, 0, mine], csend.at[0, 0], crecv.at[0, half], device
             ).start()
-            remote(
-                q_a.at[mine], r1_a.at[mine], send1.at[0], recv1.at[0], peer(z=shift, c=core)[1]
-            ).start()
+            remote(q_a.at[mine], r1_a.at[mine], send1.at[0], recv1.at[0, half], device).start()
         for u in (2, 1, 3, 0):
             for g in (1, 2):
                 if u or core:
                     slot = u * 2 + core
                     remote(
-                        q[g].at[slot, t], r1[g].at[slot, t], send1.at[g], recv1.at[g],
+                        q[g].at[slot, t], r1[g].at[slot, t], send1.at[g], recv1.at[g, half],
                         peer(**{STAGES[g][0]: u, "c": core})[1],
                     ).start()
 
+    def ship_heads(half):
+        for slot in range(1, 8):
+            for g in (1, 2):
+                remote(
+                    cs.at[half, g, slot], c1.at[half, g, slot],
+                    csend.at[g, half], crecv.at[g, half],
+                    peer(**{STAGES[g][0]: slot // 2, "c": slot % 2})[1],
+                ).start()
+
     tiles = [(g, u) for g in range(3) for u in range(4)]
 
-    def together(ahead, behind, home=False, extra=False):
+    def together(ahead, behind, home=False):
         rows = []
         done = 0
         for group in range(8):
             if ahead is not None:
                 products(*ahead, group)
-            if extra and group in (2, 5):
-                fill(1 + group // 5)
             if behind is not None:
                 upto = (group + 1) * len(tiles) // 8
                 for g, u in tiles[done:upto]:
@@ -269,23 +283,23 @@
         if behind is not None:
             ship(*behind, rows, home)
 
-    together((0, 1), None, extra=True)
+    together((0, 1), None)
 
     def step(t, carry):
         together((t, 0), (t, 1))
         together((t + 1, 1), (t, 0))
+
+        @pl.when(t == 1)
+        def _():
+            ship_heads(0)
+
         return carry
 
     lax.fori_loop(0, 3, step, 0)
     together((3, 0), (3, 1))
     together(None, (3, 0), home=True)
 
-    for slot in range(1, 8):
-        for g in (1, 2):
-            remote(
-                cs.at[g, slot], c1.at[g, slot], csend.at[g], crecv.at[g],
-                peer(**{STAGES[g][0]: slot // 2, "c": slot % 2})[1],
-            ).start()
+    ship_heads(1)
 
     def batch(src, dst, send, recv):
         return remote(src, dst, send, recv, partner)
@@ -305,36 +319,54 @@
 
     ends = [sums_first]
     others = pl.ds(1, 15)
-    for g in range(3):
-        heads = batch(cs.at[g, rest], c1.at[g, rest], csend.at[g], crecv.at[g])
-        datas = batch(q[g].at[rest], r1[g].at[rest], send1.at[g], recv1.at[g])
-        heads.wait_recv()
-        datas.wait_recv()
-        ends += [heads, datas]
-        head = [cs[g, 0]] + [c1[g, slot] for slot in range(1, 8)]
+    quarter = lax.broadcasted_iota(jnp.int32, (1, CELL), 1) // 32
+
+    def combine(g, half):
+        if g == 0:
+            slots = list(range(4 * half, 4 * half + 4))
+            n = 4 - half
+            heads, datas = c1.at[0, 0, pl.ds(4 * half, n)], r1_a.at[pl.ds(4 * half, n)]
+            pieces = [(slot, part) for slot in slots for part in range(4)]
+            own = 7
+        else:
+            slots = [slot ^ half for slot in range(8)]
+            heads = c1.at[half, g, rest]
+            datas = r1[g].at[rest, pl.ds(2 * half, 2)]
+            pieces = [(slot, 2 * half + part) for slot in slots for part in range(2)]
+            own = 0
+        batch(heads, heads, csend.at[g, 0], crecv.at[g, half]).wait_recv()
+        batch(datas, datas, send1.at[g], recv1.at[g, half]).wait_recv()
 
         def lane_row(at):
-            return jnp.concatenate(
-                [
-                    jnp.where(low, head[2 * p][at : at + 1], head[2 * p + 1][at : at + 1])
-                    for p in range(4)
-                ],
-                axis=1,
-            )
-
-        rows = lax.broadcasted_iota(jnp.int32, (256, 512), 0).astype(F32)
-        select = jnp.where(rows == lane_row(0), lane_row(1), 0.0).astype(BF16)
+            level = half if g else 0
+            rows = [
+                (cs if slot == own else c1)[level, g, slot, at : at + 1, :] for slot in slots
+            ]
+            if g == 0:
+                parts = [jnp.where(low, rows[2 * p], rows[2 * p + 1]) for p in range(2)]
+            else:
+                parts = []
+                for p in range(2):
+                    a, b, c, d = rows[4 * p : 4 * p + 4]
+                    parts.append(
+                        jnp.where(low, jnp.where(quarter == 0, a, b), jnp.where(quarter == 2, c, d))
+                    )
+            return jnp.concatenate(parts, axis=1)
+
+        targets = lax.broadcasted_iota(jnp.int32, (256, 256), 0).astype(F32)
+        select = jnp.where(targets == lane_row(0), lane_row(1), 0.0).astype(BF16)
         for row in range(ROWS[g]):
             data = jnp.concatenate(
-                [
-                    (q[g] if slot == 0 else r1[g])[slot, part, row]
-                    for slot in range(8)
-                    for part in range(4)
-                ],
-                axis=0,
+                [(q if slot == own else r1)[g][slot, part, row] for slot, part in pieces], axis=0
             )
             both = jnp.dot(select, decode(data), preferred_element_type=F32)
-            s2[g][row] = both[:, :CELL] + both[:, CELL:]
+            both = both[:, :CELL] + both[:, CELL:]
+            s2[g][row] = s2[g][row] + both if half else both
+
+    for g in range(3):
+        combine(g, 0)
+    for g in range(3):
+        combine(g, 1)
         for owner in range(16):
             scale = encode(
                 [s2[g][r, owner * 16 : owner * 16 + 16, :] for r in range(ROWS[g])],
@@ -394,6 +426,12 @@
         out_ref[:, t * CELL : (t + 1) * CELL] = filled / jnp.maximum(fraction, 0.25)
     for copy in ends:
         copy.wait_send()
+    for g in range(3):
+        mine = pl.ds(1, 7) if g else pl.ds(0, 7)
+        batch(q[g].at[mine], q[g].at[mine], send1.at[g], recv1.at[g, 0]).wait_send()
+        for half in range(2 if g else 1):
+            heads = cs.at[half, g, mine]
+            batch(heads, heads, csend.at[g, half], crecv.at[g, half]).wait_send()
 
 
 def body(fields, land_mask, intersection, send_slot, target_block, live_blocks):
@@ -406,22 +444,22 @@
     return pl.pallas_call(
         kernel,
         in_specs=[smem] + [hbm] * 5,
-        out_specs=pl.BlockSpec(memory_space=pltpu.VMEM),
-        out_shape=jax.ShapeDtypeStruct((12, TARGETS * CELL), F32),
+        out_shape=pltpu.VMEM((12, TARGETS * CELL), F32),
         scratch_shapes=[vmem((1, BLOCKS), i32), vmem((1, BLOCKS), i32)]
         + [vmem((12, BLOCKS * CELL), BF16), vmem((BLOCKS, CELL), i32)]
         + [vmem((BLOCKS, CELL, CELL), BF16), vmem((BLOCKS + 1, 16, CELL), BF16)]
         + [vmem((1, 512), i32), pltpu.SMEM((1, 512), i32)]
         + [vmem((n, CELL), F32) for n in (576, 336, 384)] * 2
         + [vmem((8, 4, r, 16, CELL), i16) for r in ROWS] * 2
-        + [vmem((3, 8, 2, CELL), F32)] * 2
+        + [vmem((2, 3, 8, 2, CELL), F32)] * 2
         + [vmem((r, 256, CELL), F32) for r in ROWS]
         + [vmem((16, r, 16, CELL), i16) for r in ROWS] * 2
         + [vmem((3, 16, 1, CELL), F32)] * 2
         + [vmem((16 * TARGETS, CELL), F32)]
         + [vmem((2, 1, CELL), F32), vmem((8, 1, CELL), F32), vmem((16, 1, CELL), F32)]
         + [dma((5,)), dma((WEIGHT_COPIES,))]
-        + [dma((3,))] * 8
+        + [dma((3,)), dma((3, 2)), dma((3, 2)), dma((3, 2))]
+        + [dma((3,))] * 4
         + [dma((2,))] * 2,
         compiler_params=pltpu.CompilerParams(
             collective_id=0, has_side_effects=True, vmem_limit_bytes=62 * 1024 * 1024

time: 34 us -> 31.8 us (0.935)
  Pallas kernels: 31.4 us -> 30.4 us
  local copies, waits for them, and re-layouts: 1.57 us -> 0.66 us
    pallas_call x1, Pallas kernels: 31.4 us -> 30.4 us  [body(): pl.pallas_call(kernel, in_specs=[smem] + [hbm] * 5, out_shape=pltpu.VMEM(...]
    unnamed x1, local copies, waits for them, and re-layouts: 1.57 us -> 0.66 us
where the time goes in v5:
time: 31.8 us; the launch traced here: 31.7 us
  Pallas kernels  30.4 us (96%)
  local copies, waits for them, and re-layouts  0.66 us (2%)
  between operations  0.66 us (2%)
    pallas_call x1, Pallas kernels, body(): pl.pallas_call(kernel, in_specs=[smem] + [hbm] * 5, out_shape=pltpu.VMEM(...  30.4 us
    unnamed x1, local copies, waits for them, and re-layouts  0.66 us

profile of v5, /device:TPU:0, one launch (start us, length us, event | category | flops | bytes accessed | tf_op | source)
XLA Modules:
  0.0 31.7 jit_solution(13978196109267135202)
XLA Ops:
  0.7 30.4 %remap.1 = f32[12,2048]{1,0:T(8,128)S(1)} custom-call(s32[1]{0:T(128)S(6)} %copy.9.live_ref, s32[1,256]{1,0:T(1,128)} %bitcast.4, s32[1,256]{1,0:T(1,128)} %bitcast.5, bf16[12,32768]{1,0:T(8,128)(2,1)} %fields_hbm.1, s32[256,128]{1,0:T(8,128)} %bitcast.3, bf16[256,128,128]{2,1,0:T(8,128)(2,1)} %weights_hbm.1), custom_call_target="tpu_custom_call" | custom-call | tf_op jit(solution)/shard_map/remap/pallas_call | solution.py:444
  31.0 0.7 %copy.8 = f32[12,2048]{1,0:T(8,128)} copy(f32[12,2048]{1,0:T(8,128)S(1)} %remap.1) | data formatting | bytes 196608

commit v6 on v5

--- a/solution.py
+++ b/solution.py
@@ -106,11 +106,8 @@
     barrier = pltpu.get_barrier_semaphore()
     greeted = set()
     for g in range(3):
-        first, second, third = STAGES[g]
         for n in range(1, 8):
-            greeted.add(tuple(sorted({first: n // 2, "c": n % 2}.items())))
-        for n in range(1, 16):
-            greeted.add(tuple(sorted({second: n // 4, third: n % 4}.items())))
+            greeted.add(tuple(sorted({STAGES[g][0]: n // 2, "c": n % 2}.items())))
     greeted = {tuple(item for item in names if item[1]) for names in greeted}
     for names in sorted(greeted):
         pl.semaphore_signal(
@@ -306,17 +303,7 @@
 
     rest = pl.ds(1, 7)
     sums_first = batch(t1.at[rest], t1.at[rest], tsend.at[0], trecv.at[0])
-    sums_first.wait_recv()
-    total = t_send[0]
-    for slot in range(1, 8):
-        total += t1[slot]
-    t_send[1] = total
     far = sorted(range(1, 16), key=lambda n: -(min(n // 4, 4 - n // 4) + min(n % 4, 4 - n % 4)))
-    for n in far:
-        remote(
-            t_send.at[1], t2.at[n], tsend.at[1], trecv.at[1], peer(x=n // 4, y=n % 4)[1]
-        ).start()
-
     ends = [sums_first]
     others = pl.ds(1, 15)
     quarter = lax.broadcasted_iota(jnp.int32, (1, CELL), 1) // 32
@@ -363,9 +350,19 @@
             both = both[:, :CELL] + both[:, CELL:]
             s2[g][row] = s2[g][row] + both if half else both
 
-    for g in range(3):
-        combine(g, 0)
-    for g in range(3):
+    for g in (1, 2, 0):
+        if g == 0:
+            sums_first.wait_recv()
+            total = t_send[0]
+            for slot in range(1, 8):
+                total += t1[slot]
+            t_send[1] = total
+            for n in far:
+                remote(
+                    t_send.at[1], t2.at[n], tsend.at[1], trecv.at[1], peer(x=n // 4, y=n % 4)[1]
+                ).start()
+        for other in {1: (1, 2), 2: (), 0: (0,)}[g]:
+            combine(other, 0)
         combine(g, 1)
         for owner in range(16):
             scale = encode(
@@ -393,7 +390,7 @@
     total = jnp.sum(jnp.where(lanes == rows, total, 0.0), axis=1, keepdims=True)
     mean = total[0:12] / jnp.maximum(total[12:13], 1.0)
     group_of = lax.broadcasted_iota(jnp.int32, (1, CELL), 1) // 16
-    for g in range(3):
+    for g in (1, 2, 0):
         heads = batch(c2.at[g, others], c2.at[g, others], c2send.at[g], c2recv.at[g])
         datas = batch(r2[g].at[others], r2[g].at[others], send2.at[g], recv2.at[g])
         heads.wait_recv()

time: 31.8 us -> 30.9 us (0.972)
  Pallas kernels: 30.4 us -> 29.2 us
    pallas_call x1, Pallas kernels: 30.4 us -> 29.2 us  [body(): pl.pallas_call(kernel, in_specs=[smem] + [hbm] * 5, out_shape=pltpu.VMEM(...]
where the time goes in v6:
time: 30.9 us; the launch traced here: 30.5 us
  Pallas kernels  29.2 us (94%)
  local copies, waits for them, and re-layouts  0.66 us (2%)
  between operations  0.66 us (2%)
    pallas_call x1, Pallas kernels, body(): pl.pallas_call(kernel, in_specs=[smem] + [hbm] * 5, out_shape=pltpu.VMEM(...  29.2 us
    unnamed x1, local copies, waits for them, and re-layouts  0.66 us

profile of v6, /device:TPU:0, one launch (start us, length us, event | category | flops | bytes accessed | tf_op | source)
XLA Modules:
  0.0 30.5 jit_solution(2251339150525191003)
XLA Ops:
  0.7 29.2 %remap.1 = f32[12,2048]{1,0:T(8,128)S(1)} custom-call(s32[1]{0:T(128)S(6)} %copy.9.live_ref, s32[1,256]{1,0:T(1,128)} %bitcast.4, s32[1,256]{1,0:T(1,128)} %bitcast.5, bf16[12,32768]{1,0:T(8,128)(2,1)} %fields_hbm.1, s32[256,128]{1,0:T(8,128)} %bitcast.3, bf16[256,128,128]{2,1,0:T(8,128)(2,1)} %weights_hbm.1), custom_call_target="tpu_custom_call" | custom-call | tf_op jit(solution)/shard_map/remap/pallas_call | solution.py:441
  29.9 0.7 %copy.8 = f32[12,2048]{1,0:T(8,128)} copy(f32[12,2048]{1,0:T(8,128)S(1)} %remap.1) | data formatting | bytes 196608

commit v7 on v6

--- a/solution.py
+++ b/solution.py
@@ -9,8 +9,8 @@
 BLOCKS = 256
 TARGETS = 16
 CHUNK = 64
-ROWS = (4, 4, 5)
-FIRST = (0, 4, 8)
+ROWS = (5, 4, 4)
+FIRST = (0, 5, 9)
 STAGES = ("zxy", "xyz", "yzx")
 SLOTS = ("zxy", "xzy", "yzx")
 MESH = pl.DeviceIdType.MESH
@@ -212,16 +212,21 @@
         for j in range(8):
             i, n = group // 2, (group % 2) * 8 + j
             value = results[j]
-            stage[0][pl.ds(i * 16 + n, 4, stride=64), :] = value[0:4]
-            stage[1][pl.ds(i * 64 + n, 4, stride=16), :] = value[4:8]
-            stage[2][pl.ds((n // 4) * 80 + i * 4 + n % 4, 5, stride=16), :] = value[8:13]
+            starts = (
+                i * 16 + n,
+                i * ROWS[1] * 16 + n,
+                (n // 4) * ROWS[2] * 16 + i * 4 + n % 4,
+            )
+            for g in range(3):
+                part = value[FIRST[g] : FIRST[g] + ROWS[g]]
+                stage[g][pl.ds(starts[g], ROWS[g], stride=16 if g else 64), :] = part
 
     def code_tile(t, core, g, u, rows):
         stage = stages[core][g]
         if g == 0:
             mine = t * 2 + 1 - core
             scale = encode(
-                [stage[r * 64 + u * 16 : r * 64 + u * 16 + 16, :] for r in range(4)],
+                [stage[r * 64 + u * 16 : r * 64 + u * 16 + 16, :] for r in range(ROWS[0])],
                 lambda r, v: q_a.__setitem__((mine, u, r), v),
             )
             rows.append(spread(scale, CHUNK, u * 16))
@@ -446,7 +451,7 @@
         + [vmem((12, BLOCKS * CELL), BF16), vmem((BLOCKS, CELL), i32)]
         + [vmem((BLOCKS, CELL, CELL), BF16), vmem((BLOCKS + 1, 16, CELL), BF16)]
         + [vmem((1, 512), i32), pltpu.SMEM((1, 512), i32)]
-        + [vmem((n, CELL), F32) for n in (576, 336, 384)] * 2
+        + [vmem((n, CELL), F32) for n in (576, 384, 384)] * 2
         + [vmem((8, 4, r, 16, CELL), i16) for r in ROWS] * 2
         + [vmem((2, 3, 8, 2, CELL), F32)] * 2
         + [vmem((r, 256, CELL), F32) for r in ROWS]

time: 30.9 us -> 30.1 us (0.974)
  Pallas kernels: 29.2 us -> 28.7 us
    pallas_call x1, Pallas kernels: 29.2 us -> 28.7 us  [body(): pl.pallas_call(kernel, in_specs=[smem] + [hbm] * 5, out_shape=pltpu.VMEM(...]
where the time goes in v7:
time: 30.1 us; the launch traced here: 30 us
  Pallas kernels  28.7 us (95%)
  local copies, waits for them, and re-layouts  0.66 us (2%)
  between operations  0.66 us (2%)
    pallas_call x1, Pallas kernels, body(): pl.pallas_call(kernel, in_specs=[smem] + [hbm] * 5, out_shape=pltpu.VMEM(...  28.7 us
    unnamed x1, local copies, waits for them, and re-layouts  0.66 us

profile of v7, /device:TPU:0, one launch (start us, length us, event | category | flops | bytes accessed | tf_op | source)
XLA Modules:
  0.0 30.0 jit_solution(15398344430058611460)
XLA Ops:
  0.7 28.7 %remap.1 = f32[12,2048]{1,0:T(8,128)S(1)} custom-call(s32[1]{0:T(128)S(6)} %copy.9.live_ref, s32[1,256]{1,0:T(1,128)} %bitcast.4, s32[1,256]{1,0:T(1,128)} %bitcast.5, bf16[12,32768]{1,0:T(8,128)(2,1)} %fields_hbm.1, s32[256,128]{1,0:T(8,128)} %bitcast.3, bf16[256,128,128]{2,1,0:T(8,128)(2,1)} %weights_hbm.1), custom_call_target="tpu_custom_call" | custom-call | tf_op jit(solution)/shard_map/remap/pallas_call | solution.py:446
  29.3 0.7 %copy.8 = f32[12,2048]{1,0:T(8,128)} copy(f32[12,2048]{1,0:T(8,128)S(1)} %remap.1) | data formatting | bytes 196608

commit v8 on v7

--- a/solution.py
+++ b/solution.py
@@ -382,6 +382,9 @@
             remote(
                 cs2.at[g, owner], c2.at[g, n], c2send.at[g], c2recv.at[g], device
             ).start()
+        for n in far:
+            at, device = peer(**{second: n // 4, third: n % 4})
+            owner = at[second] * 4 + at[third]
             remote(q2[g].at[owner], r2[g].at[n], send2.at[g], recv2.at[g], device).start()
 
     sums_second = batch(t2.at[others], t2.at[others], tsend.at[1], trecv.at[1])

time: 30.1 us -> 30.2 us (level)
  no operation moved by 1% of the time
where the time goes in v8:
time: 30.2 us; the launch traced here: 30.1 us
  Pallas kernels  28.8 us (95%)
  local copies, waits for them, and re-layouts  0.66 us (2%)
  between operations  0.66 us (2%)
    pallas_call x1, Pallas kernels, body(): pl.pallas_call(kernel, in_specs=[smem] + [hbm] * 5, out_shape=pltpu.VMEM(...  28.8 us
    unnamed x1, local copies, waits for them, and re-layouts  0.66 us

profile of v8, /device:TPU:0, one launch (start us, length us, event | category | flops | bytes accessed | tf_op | source)
XLA Modules:
  0.0 30.1 jit_solution(13062279779202093603)
XLA Ops:
  0.7 28.8 %remap.1 = f32[12,2048]{1,0:T(8,128)S(1)} custom-call(s32[1]{0:T(128)S(6)} %copy.9.live_ref, s32[1,256]{1,0:T(1,128)} %bitcast.4, s32[1,256]{1,0:T(1,128)} %bitcast.5, bf16[12,32768]{1,0:T(8,128)(2,1)} %fields_hbm.1, s32[256,128]{1,0:T(8,128)} %bitcast.3, bf16[256,128,128]{2,1,0:T(8,128)(2,1)} %weights_hbm.1), custom_call_target="tpu_custom_call" | custom-call | tf_op jit(solution)/shard_map/remap/pallas_call | solution.py:449
  29.4 0.7 %copy.8 = f32[12,2048]{1,0:T(8,128)} copy(f32[12,2048]{1,0:T(8,128)S(1)} %remap.1) | data formatting | bytes 196608
